TPU v7x, 512 devices: a whole 4x8x8 slice. The times are simulated.
512 devices in a mesh: seq: 64 (over z, y), head: 4 (over x), rep: 2 (over core).
Axes of the slice: x: 4, y: 8, z: 8, core: 2. Of those that a mesh axis runs over, the one named last changes fastest.
Arguments:
- queries: bfloat16 [16384, 8, 128], P(('rep', 'seq'), 'head'), parts along dimension 0, may hold values from -8 to 8
- keys: bfloat16 [16384, 128], P(('rep', 'seq')), parts along dimension 0, may hold values from -8 to 8
- values: bfloat16 [16384, 128], P(('rep', 'seq')), parts along dimension 0, may hold values from -6 to 6
- query_weight: float32 [16, 64, 128], P(('rep', 'head')), parts along dimension 0, may hold values from -0.075 to 0.075
- key_weight: float32 [16, 64, 128], P(('rep', 'head')), parts along dimension 0, may hold values from -0.075 to 0.075
Outputs:
- loss: float32 [2], P('rep'), parts along dimension 0
- grad_query_weight: float32 [16, 64, 128], P(('rep', 'head')), parts along dimension 0
- grad_key_weight: float32 [16, 64, 128], P(('rep', 'head')), parts along dimension 0
There are 2 independent parts, one for each index of `rep`. A program takes and returns all parts, laid end to end along the dimension named above; each array names one. Nothing has to cross between parts.
All inputs are finite; a program needn't handle non-finite values.
Results may differ from a plain program's by a relative error of at most 0.00045.
Values may be sent and summed in bfloat16 or wider, within the bound.
A program may use at most 64 MiB of HBM per device.

v0:
```python
import jax
import jax.numpy as jnp
from jax import lax
from jax.sharding import Mesh
from jax.sharding import PartitionSpec as P

WINDOW = 64
SEQ = ("seq_0", "seq_1")
REP_SEQ = ("rep", "seq_0", "seq_1")


very_low = -1e30
exact = lax.Precision.HIGHEST


def shifted(value, axis, steps):
    count = lax.axis_size(axis)
    leading, last = (max(0, -steps), min(count, count - steps))
    return lax.ppermute(value, axis, [(source, source + steps) for source in range(leading, last)])


def in_one_piece(arrays, axis, dim, along):
    ends, at = ([], 0)
    for a in arrays[:-1]:
        at += a.shape[along]
        ends.append(at)
    both = jnp.concatenate(arrays, axis=along)
    return tuple(jnp.split(lax.all_gather(both, axis, axis=dim, tiled=True), ends, axis=along))


def neutral_like(x, identity):
    return jax.tree.map(
        lambda part, zero: jnp.zeros_like(part) + jnp.asarray(zero, part.dtype), x, identity
    )


def entering(x, axes, combine, identity):
    before = start = neutral_like(x, identity)
    total = x
    for axis in reversed(axes):
        peers, place = (lax.axis_size(axis), lax.axis_index(axis))
        pieces = jax.tree.map(lambda part: lax.all_gather(part, axis), total)
        inside, total = (start, start)
        for k in reversed(range(peers)):
            passed = k > place
            total = combine(total, jax.tree.map(lambda part: part[k], pieces))
            inside = jax.tree.map(lambda new, old: jnp.where(passed, new, old), total, inside)
        before = combine(inside, before)
    return before


def filled_up(lines, peers):
    spare = -lines.shape[0] % peers
    if not spare:
        return lines
    return jnp.concatenate([lines, jnp.zeros((spare, *lines.shape[1:]), lines.dtype)])


def laid_out(tiles, dim):
    tiles = jnp.moveaxis(tiles, 0, dim)
    shape = tiles.shape
    return tiles.reshape(*shape[:dim], shape[dim] * shape[dim + 1], *shape[dim + 2 :])


def from_everyone(x, axis):
    peers = lax.axis_size(axis)
    return lax.all_to_all(jnp.broadcast_to(x[None], (peers, *x.shape)), axis, 0, 0, tiled=True)


def collect(x, axis, dim):
    return laid_out(from_everyone(x, axis), dim)


def split_up(x, dim, peers):
    shape = x.shape
    tiles = x.reshape(*shape[:dim], peers, shape[dim] // peers, *shape[dim + 1 :])
    return jnp.moveaxis(tiles, dim, 0)


def summed_on_arrival(x, axis, dim):
    peers = lax.axis_size(axis)
    tiles = lax.all_to_all(split_up(x, dim, peers), axis, 0, 0, tiled=True)
    return jnp.sum(tiles, axis=0)


def nested_sum(x, axes):
    lines = x.reshape(-1, x.shape[-1])
    padded = filled_up(lines, lax.axis_size(axes))
    whole = collect(summed_on_arrival(padded, axes, 0), axes, 0)
    return lax.slice_in_dim(whole, 0, len(lines)).reshape(x.shape)


def of_everyone(x, axis):
    everything = from_everyone(x, axis)
    return jnp.sum(everything, axis=0)


def over_axes(x, axes):
    far, near = axes
    return of_everyone(of_everyone(x, near), far)


def feature_map(act):
    first = jnp.exp(act)
    second = jnp.exp(-act)
    return jnp.concatenate(
        [
            first / jnp.sum(first, axis=-1, keepdims=True),
            second / jnp.sum(second, axis=-1, keepdims=True),
        ],
        axis=-1,
    )


def feature_back(features, grad):
    half = features.shape[-1] // 2
    first = features[..., :half]
    second = features[..., half:]
    grad_first = grad[..., :half]
    grad_second = grad[..., half:]
    return first * (grad_first - jnp.sum(first * grad_first, axis=-1, keepdims=True)) - second * (
        grad_second - jnp.sum(second * grad_second, axis=-1, keepdims=True)
    )


def key_feature_map(keys_wide, key_weight):
    return feature_map(jnp.einsum("jd,hfd->hjf", keys_wide, key_weight, precision=exact))


def add_pair(earlier, later):
    return (earlier[0] + later[0], earlier[1] + later[1])


def flash_update(carry, queries, keys, values, query_place, key_place):
    best, total, accum = carry
    scale = queries.shape[-1] ** (-0.5)
    scores = jnp.einsum("thd,jd->htj", queries, keys, preferred_element_type=jnp.float32) * scale
    allowed = (key_place[None, :] <= query_place[:, None])[None]
    scores = jnp.where(allowed, scores, very_low)
    fresh = jnp.maximum(best, jnp.max(scores, axis=-1))
    weights = jnp.where(allowed, jnp.exp(scores - fresh[..., None]), 0.0)
    total = jnp.sum(weights, axis=-1)
    accum = jnp.einsum(
        "htj,jd->htd", weights.astype(jnp.bfloat16), values, preferred_element_type=jnp.float32
    )
    return (fresh, total, accum)


def state_update(state, keys, values, key_place, bound, key_weight):

    def accumulate(inner):
        keep = (key_place < bound).astype(jnp.float32)
        features = key_feature_map(keys.astype(jnp.float32), key_weight) * keep[None, :, None]
        return (
            jnp.einsum("hjf,jd->hfd", features, values.astype(jnp.float32), precision=exact),
            jnp.sum(features, axis=1),
        )

    return lax.cond(jnp.min(key_place) < bound, accumulate, lambda inner: inner, state)


def local(queries, keys, values, query_weight, key_weight):
    rows, local_heads, width = queries.shape
    shards = lax.axis_size(SEQ)
    device = lax.axis_index(SEQ)
    feature_count = 2 * query_weight.shape[1]
    total_tokens = rows * shards
    first_place = device * rows
    bound = first_place - WINDOW
    natural_place = first_place + jnp.arange(rows, dtype=jnp.int32)
    flash_init = (
        jnp.full((local_heads, rows), very_low, jnp.float32),
        jnp.zeros((local_heads, rows), jnp.float32),
        jnp.zeros((local_heads, rows, width), jnp.float32),
    )
    zero_state = (
        jnp.zeros((local_heads, feature_count, width), jnp.float32),
        jnp.zeros((local_heads, feature_count), jnp.float32),
    )
    halo_keys, halo_values = shifted((keys[rows - WINDOW :], values[rows - WINDOW :]), SEQ, 1)
    ext_keys = jnp.concatenate([halo_keys, keys], axis=0)
    ext_values = jnp.concatenate([halo_values, values], axis=0)
    ext_count = rows + WINDOW
    ext_place = bound + jnp.arange(ext_count, dtype=jnp.int32)
    valid = ext_place >= 0
    covered = jnp.arange(ext_count, dtype=jnp.int32) < rows
    cover_mask = (valid & covered).astype(jnp.float32)
    ext_keys_wide = ext_keys.astype(jnp.float32)
    ext_values_wide = ext_values.astype(jnp.float32)
    key_features = key_feature_map(ext_keys_wide, key_weight)
    fold_keys, fold_values = (keys, values)
    piece_keys, piece_values = in_one_piece((fold_keys, fold_values), SEQ, 0, 1)
    key_place = jnp.arange(piece_keys.shape[0], dtype=jnp.int32)

    def attend(inner):
        flash = flash_update(inner[0], queries, piece_keys, piece_values, natural_place, key_place)
        state = state_update(inner[1], piece_keys, piece_values, key_place, bound, key_weight)
        return (flash, state)

    flash, folded = lax.cond(
        jnp.int32(0) < first_place + rows, attend, lambda inner: inner, (flash_init, zero_state)
    )
    teacher = jnp.transpose(flash[2] / flash[1][..., None], (1, 0, 2)).astype(jnp.bfloat16)
    scale = width ** (-0.5)
    scores = (
        jnp.einsum("thd,jd->htj", queries, ext_keys, preferred_element_type=jnp.float32) * scale
    )
    window = (
        (ext_place[None, :] <= natural_place[:, None])
        & (ext_place[None, :] > natural_place[:, None] - WINDOW)
        & valid[None, :]
    )[None]
    linear_mask = ((ext_place[None, :] <= natural_place[:, None] - WINDOW) & valid[None, :])[None]
    window_best = jnp.max(jnp.where(window, scores, very_low), axis=-1)
    window_weights = jnp.where(window, jnp.exp(scores - window_best[..., None]), 0.0)
    window_total = jnp.sum(window_weights, axis=-1)
    window_sum = jnp.einsum(
        "htj,jd->htd",
        window_weights.astype(jnp.bfloat16),
        ext_values,
        preferred_element_type=jnp.float32,
    )
    queries_wide = queries.astype(jnp.float32)
    query_features = feature_map(
        jnp.einsum("thd,hfd->htf", queries_wide, query_weight, precision=exact)
    )
    linear = jnp.where(
        linear_mask, jnp.einsum("htf,hjf->htj", query_features, key_features, precision=exact), 0.0
    )
    linear_sum = jnp.einsum("htj,jd->htd", linear, ext_values_wide, precision=exact) + jnp.einsum(
        "htf,hfd->htd", query_features, folded[0], precision=exact
    )
    linear_total = jnp.sum(linear, axis=-1) + jnp.einsum(
        "htf,hf->ht", query_features, folded[1], precision=exact
    )
    lift = jnp.exp(-window_best)
    denominator = window_total + lift * linear_total
    student = (window_sum + lift[..., None] * linear_sum) / denominator[..., None]
    teacher_wide = jnp.transpose(teacher, (1, 0, 2)).astype(jnp.float32)
    difference = student - teacher_wide
    loss_part = jnp.sum(difference * difference) / total_tokens
    grad_out = 2.0 * difference / total_tokens
    num_grad = lift[..., None] * grad_out / denominator[..., None]
    den_grad = -lift * jnp.sum(grad_out * student, axis=-1) / denominator
    adjoint = (
        jnp.einsum("htf,htd->hfd", query_features, num_grad, precision=exact),
        jnp.einsum("htf,ht->hf", query_features, den_grad, precision=exact),
    )
    later = entering(adjoint, SEQ, add_pair, zero_state)
    link = jnp.where(
        linear_mask,
        jnp.einsum("htd,jd->htj", num_grad, ext_values_wide, precision=exact) + den_grad[..., None],
        0.0,
    )
    query_feature_grad = (
        jnp.einsum("htj,hjf->htf", link, key_features, precision=exact)
        + jnp.einsum("htd,hfd->htf", num_grad, folded[0], precision=exact)
        + den_grad[..., None] * folded[1][:, None, :]
    )
    key_feature_grad = (
        jnp.einsum("htj,htf->hjf", link, query_features, precision=exact)
        + jnp.einsum("jd,hfd->hjf", ext_values_wide, later[0], precision=exact)
        + later[1][:, None, :]
    )
    key_feature_grad = key_feature_grad * cover_mask[None, :, None]
    query_act_grad = feature_back(query_features, query_feature_grad)
    key_act_grad = feature_back(key_features, key_feature_grad)
    grad_query = jnp.einsum("htf,thd->hfd", query_act_grad, queries_wide, precision=exact)
    grad_key = jnp.einsum("hjf,jd->hfd", key_act_grad, ext_keys_wide, precision=exact)
    grad_query, grad_key = (nested_sum(grad_query, SEQ), nested_sum(grad_key, SEQ))
    loss = over_axes(loss_part, (("seq_0", "seq_1"), "head")).reshape(1)
    return (loss, grad_query, grad_key)


def solution(mesh):
    split = Mesh(
        mesh.devices.reshape(8, 8, mesh.shape["head"], mesh.shape["rep"]),
        ("seq_0", "seq_1", "head", "rep"),
    )
    return jax.shard_map(
        local,
        mesh=split,
        in_specs=(
            P(REP_SEQ, "head", None),
            P(REP_SEQ, None),
            P(REP_SEQ, None),
            P(("rep", "head"), None, None),
            P(("rep", "head"), None, None),
        ),
        out_specs=(P("rep"), P(("rep", "head"), None, None), P(("rep", "head"), None, None)),
        check_vma=False,
    )
```

profile of v0, /device:TPU:6, one launch (start us, length us, event | category | flops | bytes accessed | tf_op | source)
XLA Modules:
  0.0 313.4 jit_solution(10058284865789060797)
XLA Ops:
  9.4 3.5 %collective-permute-start = (bf16[64,128]{1,0:T(8,128)(2,1)S(1)}, bf16[64,128]{1,0:T(8,128)(2,1)S(1)}, u32[]{:S(2)}, u32[]{:S(2)}) collective-permute-start(bf16[64,128]{1,0:T(8,128)(2,1)S(1)} %slice.114), channel_id=1, source_target_pairs={{0,8},{8,16},{16,24},{24,32},{32,40},{40,48},{48,56},{56,64},{64,7... | collective-permute-start | bytes 49160 | tf_op jit(solution)/shard_map/ppermute | solution.py:19
  13.6 3.5 %collective-permute-start.1 = (bf16[64,128]{1,0:T(8,128)(2,1)S(1)}, bf16[64,128]{1,0:T(8,128)(2,1)S(1)}, u32[]{:S(2)}, u32[]{:S(2)}) collective-permute-start(bf16[64,128]{1,0:T(8,128)(2,1)S(1)} %slice.115), channel_id=1, source_target_pairs={{0,8},{8,16},{16,24},{24,32},{32,40},{40,48},{48,56},{56,64},{64,7... | collective-permute-start | bytes 49160 | tf_op jit(solution)/shard_map/ppermute | solution.py:19
  21.4 81.6 %all-gather.7.cloned.1.call-done = bf16[8192,256]{1,0:T(8,128)(2,1)} async-done(((bf16[128,256]{1,0:T(8,128)(2,1)}), bf16[8192,256]{1,0:T(8,128)(2,1)}) %all-gather.7.cloned.1.call-update) | async-done | bytes 4194320 | tf_op jit(solution)/shard_map/all_gather | solution.py:28
  103.1 14.9 %conditional.2 = (f32[2,128]{1,0:T(2,128)S(1)}, f32[2,128,128]{2,1,0:T(8,128)}, f32[2,128]{1,0:T(2,128)}, f32[2,128,128]{1,2,0:T(8,128)S(1)}) conditional(s32[]{:T(128)} %convert_element_type.35, () %tuple.24, (s32[8192]{0:T(1024)S(1)}, s32[]{:T(128)}, s32[128]{0:T(128)S(1)}, bf16[8192,256]{1,0:T(8,128)(2,1)}, bf16[128,2,128]{2,1,0:T(2,128)(2,1)}, ...), branch_computations={%region_5.0_spmd, %region_6.15_spmd} | conditional | flops 5942272000 | bytes 105980616 | solution.py:200
  103.1 3.7 %broadcast_compare_fusion = pred[128,8192]{0,1:T(8,128)(4,1)S(1)} fusion(s32[128]{0:T(128)S(1)} %broadcast_add_fusion, s32[8192]{0:T(1024)S(1)} %get-tuple-element.44), kind=kLoop, calls=%fused_computation.26 | loop fusion | flops 1048576 | bytes 1081856 | tf_op jit(solution)/shard_map/cond/branch_1_fun/le | solution.py:138
  106.8 3.5 %fusion.131 = (f32[2,128]{1,0:T(2,128)S(1)}, f32[2,128,8192]{1,2,0:T(8,128)S(1)}) fusion(bf16[128,2,128]{2,1,0:T(2,128)(2,1)} %get-tuple-element.89, bf16[8192,256]{1,0:T(8,128)(2,1)} %get-tuple-element.39, pred[128,8192]{0,1:T(8,128)(4,1)S(1)} %broadcast_compare_fusion), kind=kOutput, calls=%fused_computation.212 | convolution fusion | flops 543162112 | bytes 11600896 | tf_op jit(solution)/shard_map/cond/branch_1_fun/thd,jd->htj/dot_general | solution.py:137
  110.3 1.7 fusion.11
  112.1 1.7 fusion.10
  122.5 46.7 %all-gather.11.cloned.1.call-done = f32[16,128,128]{2,1,0:T(8,128)} async-done(((f32[2,128,128]{2,1,0:T(8,128)}), f32[16,128,128]{2,1,0:T(8,128)}) %all-gather.11.cloned.1.call-update) | async-done | bytes 1048592 | tf_op jit(solution)/shard_map/all_gather | solution.py:42
  169.2 2.0 fusion.36
  172.8 4.8 %all-to-all-start = ((f32[4,1,1]{2,1,0:T(1,128)}), f32[4,1,1]{2,1,0:T(1,128)S(1)}, u32[]{:S(2)}, u32[]{:S(2)}) async-start(f32[4,1,1]{2,1,0:T(1,128)} %broadcast_in_dim.68), calls=%async_computation | async-start | bytes 4096 | tf_op jit(solution)/shard_map/all_to_all | solution.py:67
  177.5 15.0 %all-gather.2 = f32[8,2,128]{2,1,0:T(2,128)S(1)} all-gather(f32[1,2,128]{2,1,0:T(2,128)S(1)} %bitcast.141), channel_id=3, replica_groups=mesh['seq_0'=8,'seq_1'=8,'head'=4,'rep'=2] {'seq_1'}, dimensions={0}, use_global_device_ids=true | all-gather | bytes 9216 | tf_op jit(solution)/shard_map/all_gather | solution.py:42
  192.5 17.3 %all_gather.29 = f32[8,2,128]{2,1,0:T(2,128)S(1)} all-gather(f32[1,2,128]{2,1,0:T(2,128)S(1)} %get-tuple-element.107), channel_id=1, replica_groups=mesh['seq_0'=8,'seq_1'=8,'head'=4,'rep'=2] {'seq_0'}, dimensions={0}, use_global_device_ids=true | all-gather | bytes 9216 | tf_op jit(solution)/shard_map/all_gather | solution.py:42
  215.7 9.0 %all-to-all-start.1 = ((f32[64,1,1]{2,1,0:T(1,128)}), f32[64,1,1]{2,1,0:T(1,128)S(1)}, u32[]{:S(2)}, u32[]{:S(2)}) async-start(f32[64,1,1]{2,1,0:T(1,128)} %broadcast_in_dim.69), calls=%async_computation.1 | async-start | bytes 65536 | tf_op jit(solution)/shard_map/all_to_all | solution.py:67
  224.7 1.9 fusion.24
  226.6 10.0 %all-to-all-done.1 = f32[64,1,1]{2,1,0:T(1,128)S(1)} async-done(((f32[64,1,1]{2,1,0:T(1,128)}), f32[64,1,1]{2,1,0:T(1,128)S(1)}, u32[]{:S(2)}, u32[]{:S(2)}) %all-to-all-start.1) | async-done | bytes 288 | tf_op jit(solution)/shard_map/all_to_all | solution.py:67
  236.6 4.6 %all-to-all-start.2 = ((f32[64,2,128]{2,1,0:T(2,128)}), f32[64,2,128]{2,1,0:T(2,128)S(1)}, u32[]{:S(2)}, u32[]{:S(2)}) async-start(f32[64,2,128]{2,1,0:T(2,128)} %bitcast.17), calls=%async_computation.2 | async-start | bytes 131072 | tf_op jit(solution)/shard_map/all_to_all | solution.py:82
  242.1 11.4 %all-to-all-done.2 = f32[64,2,128]{2,1,0:T(2,128)S(1)} async-done(((f32[64,2,128]{2,1,0:T(2,128)}), f32[64,2,128]{2,1,0:T(2,128)S(1)}, u32[]{:S(2)}, u32[]{:S(2)}) %all-to-all-start.2) | async-done | bytes 65568 | tf_op jit(solution)/shard_map/all_to_all | solution.py:82
  253.5 4.6 %all-to-all-start.4 = ((f32[64,2,128]{2,1,0:T(2,128)}), f32[64,2,128]{2,1,0:T(2,128)S(1)}, u32[]{:S(2)}, u32[]{:S(2)}) async-start(f32[64,2,128]{2,1,0:T(2,128)} %bitcast.34), calls=%async_computation.4 | async-start | bytes 131072 | tf_op jit(solution)/shard_map/all_to_all | solution.py:82
  258.2 12.4 %all-to-all-done.4 = f32[64,2,128]{2,1,0:T(2,128)S(1)} async-done(((f32[64,2,128]{2,1,0:T(2,128)}), f32[64,2,128]{2,1,0:T(2,128)S(1)}, u32[]{:S(2)}, u32[]{:S(2)}) %all-to-all-start.4) | async-done | bytes 65568 | tf_op jit(solution)/shard_map/all_to_all | solution.py:82
  271.3 4.6 %all-to-all-start.3 = ((f32[64,2,128]{2,1,0:T(2,128)}), f32[64,2,128]{2,1,0:T(2,128)S(1)}, u32[]{:S(2)}, u32[]{:S(2)}) async-start(f32[64,2,128]{2,1,0:T(2,128)} %broadcast_in_dim.70), calls=%async_computation.3 | async-start | bytes 131072 | tf_op jit(solution)/shard_map/all_to_all | solution.py:67
  276.0 12.2 %all-to-all-done.3 = f32[64,2,128]{2,1,0:T(2,128)S(1)} async-done(((f32[64,2,128]{2,1,0:T(2,128)}), f32[64,2,128]{2,1,0:T(2,128)S(1)}, u32[]{:S(2)}, u32[]{:S(2)}) %all-to-all-start.3) | async-done | bytes 65568 | tf_op jit(solution)/shard_map/all_to_all | solution.py:67
  288.8 4.6 %all-to-all-start.5 = ((f32[64,2,128]{2,1,0:T(2,128)}), f32[64,2,128]{2,1,0:T(2,128)S(1)}, u32[]{:S(2)}, u32[]{:S(2)}) async-start(f32[64,2,128]{2,1,0:T(2,128)} %broadcast_in_dim.71), calls=%async_computation.5 | async-start | bytes 131072 | tf_op jit(solution)/shard_map/all_to_all | solution.py:67
  294.1 11.6 %all-to-all-done.5 = f32[64,2,128]{2,1,0:T(2,128)S(1)} async-done(((f32[64,2,128]{2,1,0:T(2,128)}), f32[64,2,128]{2,1,0:T(2,128)S(1)}, u32[]{:S(2)}, u32[]{:S(2)}) %all-to-all-start.5) | async-done | bytes 65568 | tf_op jit(solution)/shard_map/all_to_all | solution.py:67
  (74 shorter events, 27.3 us)
Async XLA Ops:
  7.2 10.0 %copy-start = (f32[2,64,128]{2,1,0:T(8,128)S(1)}, f32[2,64,128]{2,1,0:T(8,128)}, u32[]{:S(2)}) copy-start(f32[2,64,128]{2,1,0:T(8,128)} %param.12) | copy-start | bytes 196612
  7.2 95.9 %all-gather.7.cloned.1.call-start = ((), (), s32[]{:S(2)}) async-start(), calls=%async_computation.6 | async-start | bytes 4259840 | tf_op jit(solution)/shard_map/all_gather | solution.py:28
  8.7 160.5 %all-gather.11.cloned.1.call-start = ((), (), s32[]{:S(2)}) async-start(), calls=%async_computation.8 | async-start | bytes 1179648 | tf_op jit(solution)/shard_map/all_gather | solution.py:42
  9.4 9.0 %collective-permute-start = (bf16[64,128]{1,0:T(8,128)(2,1)S(1)}, bf16[64,128]{1,0:T(8,128)(2,1)S(1)}, u32[]{:S(2)}, u32[]{:S(2)}) collective-permute-start(bf16[64,128]{1,0:T(8,128)(2,1)S(1)} %slice.114), channel_id=1, source_target_pairs={{0,8},{8,16},{16,24},{24,32},{32,40},{40,48},{48,56},{56,64},{64,7... | collective-permute-start | bytes 49160 | tf_op jit(solution)/shard_map/ppermute | solution.py:19
  13.6 106.5 %collective-permute-start.1 = (bf16[64,128]{1,0:T(8,128)(2,1)S(1)}, bf16[64,128]{1,0:T(8,128)(2,1)S(1)}, u32[]{:S(2)}, u32[]{:S(2)}) collective-permute-start(bf16[64,128]{1,0:T(8,128)(2,1)S(1)} %slice.115), channel_id=1, source_target_pairs={{0,8},{8,16},{16,24},{24,32},{32,40},{40,48},{48,56},{56,64},{64,7... | collective-permute-start | bytes 49160 | tf_op jit(solution)/shard_map/ppermute | solution.py:19
  103.1 17.1 %copy-start.6 = (bf16[128,128]{1,0:T(8,128)(2,1)S(1)}, bf16[128,128]{1,0:T(8,128)(2,1)}, u32[]{:S(2)}) copy-start(bf16[128,128]{1,0:T(8,128)(2,1)} %param.11) | copy-start | bytes 98308
  106.8 3.5 %copy-start.1 = (bf16[8192,256]{1,0:T(8,128)(2,1)S(1)}, bf16[8192,256]{1,0:T(8,128)(2,1)}, u32[]{:S(2)}) copy-start(bf16[8192,256]{1,0:T(8,128)(2,1)} %get-tuple-element.39) | copy-start | bytes 12582916 | tf_op jit(solution)/shard_map/cond
  113.8 2.9 copy-start.4
  117.9 94.5 %copy-start.5 = (bf16[128,2,128]{2,1,0:T(2,128)(2,1)S(1)}, bf16[128,2,128]{2,1,0:T(2,128)(2,1)}, u32[]{:S(2)}) copy-start(bf16[128,2,128]{2,1,0:T(2,128)(2,1)} %param.9) | copy-start | bytes 196612
  121.3 119.9 %copy-start.3 = (bf16[128,128]{1,0:T(8,128)(2,1)S(1)}, bf16[128,128]{1,0:T(8,128)(2,1)}, u32[]{:S(2)}) copy-start(bf16[128,128]{1,0:T(8,128)(2,1)} %param.10) | copy-start | bytes 98308
  122.4 102.3 %all-gather.9.cloned.1.call-start = ((), (), s32[]{:S(2)}) async-start(), calls=%async_computation.7 | async-start | bytes 1179648 | tf_op jit(solution)/shard_map/all_gather | solution.py:42
  172.8 41.0 %all-to-all-start = ((f32[4,1,1]{2,1,0:T(1,128)}), f32[4,1,1]{2,1,0:T(1,128)S(1)}, u32[]{:S(2)}, u32[]{:S(2)}) async-start(f32[4,1,1]{2,1,0:T(1,128)} %broadcast_in_dim.68), calls=%async_computation | async-start | bytes 4096 | tf_op jit(solution)/shard_map/all_to_all | solution.py:67
  215.7 20.9 %all-to-all-start.1 = ((f32[64,1,1]{2,1,0:T(1,128)}), f32[64,1,1]{2,1,0:T(1,128)S(1)}, u32[]{:S(2)}, u32[]{:S(2)}) async-start(f32[64,1,1]{2,1,0:T(1,128)} %broadcast_in_dim.69), calls=%async_computation.1 | async-start | bytes 65536 | tf_op jit(solution)/shard_map/all_to_all | solution.py:67
  236.6 16.9 %all-to-all-start.2 = ((f32[64,2,128]{2,1,0:T(2,128)}), f32[64,2,128]{2,1,0:T(2,128)S(1)}, u32[]{:S(2)}, u32[]{:S(2)}) async-start(f32[64,2,128]{2,1,0:T(2,128)} %bitcast.17), calls=%async_computation.2 | async-start | bytes 131072 | tf_op jit(solution)/shard_map/all_to_all | solution.py:82
  253.5 17.1 %all-to-all-start.4 = ((f32[64,2,128]{2,1,0:T(2,128)}), f32[64,2,128]{2,1,0:T(2,128)S(1)}, u32[]{:S(2)}, u32[]{:S(2)}) async-start(f32[64,2,128]{2,1,0:T(2,128)} %bitcast.34), calls=%async_computation.4 | async-start | bytes 131072 | tf_op jit(solution)/shard_map/all_to_all | solution.py:82
  271.3 16.9 %all-to-all-start.3 = ((f32[64,2,128]{2,1,0:T(2,128)}), f32[64,2,128]{2,1,0:T(2,128)S(1)}, u32[]{:S(2)}, u32[]{:S(2)}) async-start(f32[64,2,128]{2,1,0:T(2,128)} %broadcast_in_dim.70), calls=%async_computation.3 | async-start | bytes 131072 | tf_op jit(solution)/shard_map/all_to_all | solution.py:67
  288.8 16.9 %all-to-all-start.5 = ((f32[64,2,128]{2,1,0:T(2,128)}), f32[64,2,128]{2,1,0:T(2,128)S(1)}, u32[]{:S(2)}, u32[]{:S(2)}) async-start(f32[64,2,128]{2,1,0:T(2,128)} %broadcast_in_dim.71), calls=%async_computation.5 | async-start | bytes 131072 | tf_op jit(solution)/shard_map/all_to_all | solution.py:67
Sparse Core Ops, SparseCore 0:
  11.6 91.3 all-gather.6
  122.5 46.6 all-gather.10
  171.3 40.8 all-gather.8
where the time goes:
time: 314 us; the launch traced here: 313 us
  waiting for transfers between devices  186 us (59%)
  starting transfers between devices  39.3 us (13%)
  blocking collectives  32.3 us (10%)
  matrix products  20.4 us (6%)
  between operations  14.7 us (5%)
  other arithmetic  11.3 us (4%)
  local copies, waits for them, and re-layouts  8.71 us (3%)
    all_gather x1, waiting for transfers between devices, in_one_piece(): lax.all_gather(both, axis, axis=dim, tiled=True)  81.6 us
    all_gather x2, waiting for transfers between devices, entering(): pieces = jax.tree.map(lambda part: lax.all_gather(part, axis), total)  46.7 us
    all_to_all x4, waiting for transfers between devices, from_everyone(): lax.all_to_all(jnp.broadcast_to(x[None], (peers, *x.shape)), axis, 0, 0,...  33.7 us
    all_gather x2, blocking collectives, entering(): pieces = jax.tree.map(lambda part: lax.all_gather(part, axis), total)  32.3 us
    all_to_all x2, waiting for transfers between devices, summed_on_arrival(): tiles = lax.all_to_all(split_up(x, dim, peers), axis, 0, 0, tiled=True)  23.9 us
    all_to_all x4, starting transfers between devices, from_everyone(): lax.all_to_all(jnp.broadcast_to(x[None], (peers, *x.shape)), axis, 0, 0,...  23 us
    all_to_all x2, starting transfers between devices, summed_on_arrival(): tiles = lax.all_to_all(split_up(x, dim, peers), axis, 0, 0, tiled=True)  9.23 us
    ppermute x2, starting transfers between devices, shifted(): lax.ppermute(value, axis, [(source, source + steps) for source in range(l...  6.94 us
  transfers between devices with their start and end apart: 11, of which 7 were waited for; matrix products, arithmetic and copies ran while one was open for 10% of the time, Pallas kernels for 0%

commit v1 on v0

v1 whole, which is shorter than its diff:
```python
import functools

import jax
import jax.numpy as jnp
from jax import lax
from jax.experimental import pallas as pl
from jax.experimental.pallas import tpu as pltpu
from jax.sharding import Mesh
from jax.sharding import PartitionSpec as P

WINDOW = 64
Z, Y, X = "seq_0", "seq_1", "head"
REP_SEQ = ("rep", Z, Y)
MESH = pl.DeviceIdType.MESH
RING = 8
LOW = -1e30
F32 = jnp.float32
BF16 = jnp.bfloat16
CHUNK = 4
FAR_FIRST = (4, 3, 5, 2, 6, 1, 7)


def around(place, steps):
    return lax.rem(place + (steps + RING), RING)


def remote(src, dst, send, recv, axis, place):
    return pltpu.make_async_remote_copy(
        src_ref=src,
        dst_ref=dst,
        send_sem=send,
        recv_sem=recv,
        device_id={axis: place},
        device_id_type=MESH,
    )


def greet(peers):
    barrier = pltpu.get_barrier_semaphore()
    for axis, place in peers:
        pl.semaphore_signal(barrier, inc=1, device_id={axis: place}, device_id_type=MESH)
    pl.semaphore_wait(barrier, len(peers))


def gather_kernel(k_ref, v_ref, kb, vb, send_sems, k_recv, v_recv):
    z, y = lax.axis_index(Z), lax.axis_index(Y)
    greet([(Z, around(z, 1)), (Z, around(z, -1)), (Y, around(y, 1)), (Y, around(y, -1))])
    place = {Z: z, Y: y}
    streams = (
        (k_ref, kb, send_sems.at[0], k_recv, Y, Z),
        (v_ref, vb, send_sems.at[1], v_recv, Z, Y),
    )

    def index(stream, along, across):
        at = {stream[4]: around(place[stream[4]], along), stream[5]: around(place[stream[5]], across)}
        return at[Z] * RING + at[Y]

    def send(stream, src, at, axis, step):
        remote(src, stream[1].at[at], stream[2], stream[3].at[at], axis, around(place[axis], step)).start()

    def arrived(stream, at):
        block = stream[1].at[at]
        remote(block, block, stream[2], stream[3].at[at], Z, z).wait_recv()

    for stream in streams:
        own = index(stream, 0, 0)
        for axis in (stream[4], stream[5]):
            send(stream, stream[0], own, axis, 1)
            send(stream, stream[0], own, axis, -1)
    for stream in streams:
        stream[1][index(stream, 0, 0)] = stream[0][...]
    for hop in range(1, 5):
        for way in (1, -1):
            if hop == 4 and way == -1:
                continue
            for stream in streams:
                at = index(stream, -way * hop, 0)
                arrived(stream, at)
                if hop < (4 if way == 1 else 3):
                    send(stream, stream[1].at[at], at, stream[4], way)
                send(stream, stream[1].at[at], at, stream[5], 1)
                send(stream, stream[1].at[at], at, stream[5], -1)
    for hop in range(1, 5):
        for along in (0, -1, 1, -2, 2, -3, 3, 4):
            for way in (1, -1):
                last = (way == 1) == (along % 2 == 0)
                if hop == 4 and not last:
                    continue
                for stream in streams:
                    at = index(stream, along, -way * hop)
                    arrived(stream, at)
                    if hop < 3 or (hop == 3 and last):
                        send(stream, stream[1].at[at], at, stream[5], way)
    for stream in streams:
        sent = stream[1].at[pl.ds(0, RING * RING - 1)]
        remote(sent, sent, stream[2], stream[3].at[0], Z, z).wait_send()


VMEM = pl.BlockSpec(memory_space=pltpu.VMEM)


def gather(keys, values):
    blocks = jax.ShapeDtypeStruct((RING * RING, *keys.shape), BF16)
    return pl.pallas_call(
        gather_kernel,
        out_shape=(blocks, blocks),
        in_specs=[VMEM] * 2,
        out_specs=(VMEM, VMEM),
        scratch_shapes=[
            pltpu.SemaphoreType.DMA((2,)),
            pltpu.SemaphoreType.DMA((RING * RING,)),
            pltpu.SemaphoreType.DMA((RING * RING,)),
        ],
        compiler_params=pltpu.CompilerParams(collective_id=0, has_side_effects=True),
        name="gather_kv",
    )(keys, values)


def exchange_kernel(scan, rows, tile, *refs):
    if tile:
        x_ref, tile_ref, out, tile_out, b1, t, b2, o, tiles, send, r1, r2, r3, rt = refs
    else:
        x_ref, out, b1, t, b2, o, send, r1, r2, r3 = refs
    z, y = lax.axis_index(Z), lax.axis_index(Y)
    peers = [(Y, around(y, d)) for d in FAR_FIRST] + [(Z, around(z, d)) for d in FAR_FIRST]
    if tile:
        x = lax.axis_index(X)
        others = [lax.rem(x + d, 4) for d in (2, 1, 3)]
        peers += [(X, p) for p in others]
    greet(peers)
    for d in FAR_FIRST:
        p = around(y, d)
        remote(x_ref.at[p], b1.at[y], send.at[0], r1.at[y], Y, p).start()
    if tile:
        for p in others:
            remote(tile_ref, tiles.at[x], send.at[3], rt.at[x], X, p).start()
    b1[y] = x_ref[y]
    for d in (1, 7, 2, 6, 3, 5, 4):
        p = around(y, d)
        remote(b1.at[p], b1.at[p], send.at[0], r1.at[p], Y, p).wait_recv()
    total = b1[0]
    for k in range(1, RING):
        total = total + b1[k]
    t[...] = total
    for d in FAR_FIRST:
        p = around(z, d)
        remote(t, b2.at[z], send.at[1], r2.at[z], Z, p).start()
    b2[z] = total
    for d in (1, 7, 2, 6, 3, 5, 4):
        p = around(z, d)
        remote(b2.at[p], b2.at[p], send.at[1], r2.at[p], Z, p).wait_recv()
    if scan:
        base = jnp.zeros((scan, 128), F32)
        for k in range(RING):
            base = base + jnp.where(k > z, b2[k, :scan], 0.0)
        for k in reversed(range(RING)):
            o[k, :scan] = base
            base = base + b1[k, :scan]
    total = b2[0, scan:]
    for k in range(1, RING):
        total = total + b2[k, scan:]
    for k in range(RING):
        o[k, scan:] = total
    for d in FAR_FIRST:
        p = around(y, d)
        remote(o.at[p], out.at[y], send.at[2], r3.at[y], Y, p).start()
    out[y] = o[y]
    if tile:
        tiles[x] = tile_ref[...]
        for p in others:
            remote(tile_ref, tiles.at[p], send.at[3], rt.at[p], X, p).wait_recv()
        tile_out[...] = tiles[0] + tiles[1] + tiles[2] + tiles[3]
    for d in (1, 7, 2, 6, 3, 5, 4):
        p = around(y, d)
        remote(out.at[p], out.at[p], send.at[2], r3.at[p], Y, p).wait_recv()
    most = x_ref.at[pl.ds(0, RING - 1)]
    for k in range(3):
        remote(most, most, send.at[k], r1.at[0], Y, y).wait_send()
    if tile:
        three = tiles.at[pl.ds(0, 3)]
        remote(three, three, send.at[3], r1.at[0], Y, y).wait_send()


def exchange(x, scan, collective_id, tile=None):
    rows = x.shape[1]
    full = pltpu.VMEM((RING, rows, 128), F32)
    dma = pltpu.SemaphoreType.DMA
    scratch = [full, pltpu.VMEM((rows, 128), F32), full, full]
    sems = [dma((4,)), dma((RING,)), dma((RING,)), dma((RING,))]
    outs = [jax.ShapeDtypeStruct(x.shape, F32)]
    args = [x]
    if tile is not None:
        scratch.append(pltpu.VMEM((4, 8, 128), F32))
        sems.append(dma((4,)))
        outs.append(jax.ShapeDtypeStruct((8, 128), F32))
        args.append(tile)
    return pl.pallas_call(
        functools.partial(exchange_kernel, scan, rows, tile is not None),
        out_shape=tuple(outs),
        in_specs=[VMEM] * len(args),
        out_specs=(VMEM,) * len(outs),
        scratch_shapes=scratch + sems,
        compiler_params=pltpu.CompilerParams(collective_id=collective_id, has_side_effects=True),
        name="exchange",
    )(*args)


NN = (((1,), (0,)), ((), ()))
NT = (((1,), (1,)), ((), ()))


def dot(a, b, dims=NN):
    return lax.dot_general(a, b, dims, preferred_element_type=F32)


def two(a):
    high = a.astype(BF16)
    return high, (a - high.astype(F32)).astype(BF16)


def dot_wide(a, b, dims=NN):
    a_high, a_low = two(a)
    b_high, b_low = two(b)
    return dot(a_high, b_high, dims) + (dot(a_high, b_low, dims) + dot(a_low, b_high, dims))


def dot_left(a, b, dims=NN):
    high, low = two(a)
    return dot(high, b, dims) + dot(low, b, dims)


def dot_right(a, b, dims=NN):
    high, low = two(b)
    return dot(a, high, dims) + dot(a, low, dims)


def three(a):
    high = a.astype(BF16)
    rest = a - high.astype(F32)
    mid = rest.astype(BF16)
    return high, mid, (rest - mid.astype(F32)).astype(BF16)


def features_of(pieces, tokens):
    act = dot(pieces[0], tokens, NT) + (dot(pieces[1], tokens, NT) + dot(pieces[2], tokens, NT))
    half = 64
    parts = []
    for h in range(act.shape[0] // half):
        one = act[h * half : (h + 1) * half]
        for e in (jnp.exp(one), jnp.exp(-one)):
            parts.append(e * (1.0 / jnp.sum(e, axis=0, keepdims=True)))
    return jnp.concatenate(parts, axis=0)


def features_back(features, grad):
    half = features.shape[0] // 2
    p, r = features[:half], features[half:]
    dp, dr = grad[:half], grad[half:]
    return p * (dp - jnp.sum(p * dp, axis=0, keepdims=True)) - r * (
        dr - jnp.sum(r * dr, axis=0, keepdims=True)
    )


def iota(shape, axis):
    return lax.broadcasted_iota(jnp.int32, shape, axis)


def attend_kernel(
    q_ref, kb, vb, wq_ref, wk_ref,
    x_out, tile_out, kf_out, kfg_out, kext_out, vext_out,
    scores, best, state, state_sum, total, accum,
):
    z, y = lax.axis_index(Z), lax.axis_index(Y)
    me = z * RING + y
    rows = 128
    tokens = rows * RING * RING
    first = me * rows
    bound = first - WINDOW
    scale = 128 ** (-0.5)
    q_all = q_ref[...].reshape(2 * rows, 128)
    wide = CHUNK * rows
    count = me // CHUNK + 1
    wk = three(wk_ref[...].reshape(128, 128))

    best[...] = jnp.full(best.shape, LOW, F32)
    state[...] = jnp.zeros_like(state)
    state_sum[...] = jnp.zeros_like(state_sum)
    total[...] = jnp.zeros_like(total)
    accum[...] = jnp.zeros_like(accum)

    query_place = first + jnp.bitwise_and(iota((2 * rows, wide), 0), rows - 1)
    lane = iota((2 * rows, wide), 1)

    def lanes(fold, start, value):
        for k in range(CHUNK):
            start = fold(start, value[:, k * 128 : (k + 1) * 128])
        return start

    @pl.loop(0, count)
    def _(c):
        kc = kb[pl.ds(c * CHUNK, CHUNK)].reshape(wide, 128)
        vc = vb[pl.ds(c * CHUNK, CHUNK)].reshape(wide, 128)
        s = dot(q_all, kc, NT) * scale
        s = jnp.where(lane + c * wide <= query_place, s, LOW)
        scores[c] = s
        best[...] = lanes(jnp.maximum, best[...], s)
        f = features_of(wk, kc)
        f = jnp.where(lane + c * wide < bound, f, 0.0)
        state_sum[...] = lanes(jnp.add, state_sum[...], f)
        state[...] += dot_left(f, vc)

    top = jnp.max(best[...], axis=1, keepdims=True)

    @pl.loop(0, count)
    def _(c):
        vc = vb[pl.ds(c * CHUNK, CHUNK)].reshape(wide, 128)
        w = jnp.exp(scores[c] - top)
        total[...] = lanes(jnp.add, total[...], w)
        accum[...] += dot(w.astype(BF16), vc)

    teacher = accum[...] / jnp.sum(total[...], axis=1, keepdims=True)
    teacher = teacher.astype(BF16).astype(F32)

    before = jnp.maximum(me - 1, 0)
    kext = jnp.concatenate([kb[before], kb[me]], axis=0)
    vext = jnp.concatenate([vb[before], vb[me]], axis=0)
    kf_all = features_of(wk, kext)
    kf_out[...] = kf_all
    kext_out[...] = kext
    vext_out[...] = vext
    span = 2 * rows
    t_place = first + iota((rows, span), 0)
    j_place = first - rows + iota((rows, span), 1)
    window = (j_place <= t_place) & (j_place > t_place - WINDOW) & (j_place >= 0)
    linear_mask = (j_place <= t_place - WINDOW) & (j_place >= bound) & (j_place >= 0)
    t_turned = first + iota((span, rows), 1)
    j_turned = first - rows + iota((span, rows), 0)
    turned_mask = (j_turned <= t_turned - WINDOW) & (j_turned >= bound) & (j_turned >= 0)

    loss = jnp.zeros((8, 128), F32)
    rows_of_a = []
    for h in range(2):
        q = q_ref[h]
        s = dot(q, kext, NT) * scale
        window_best = jnp.max(jnp.where(window, s, LOW), axis=1, keepdims=True)
        weights = jnp.where(window, jnp.exp(s - window_best), 0.0)
        window_total = jnp.sum(weights, axis=1, keepdims=True)
        window_sum = dot(weights.astype(BF16), vext)
        qft = features_of(three(wq_ref[h]), q)
        qf = qft.T
        kft = kf_all[h * 128 : (h + 1) * 128]
        prefix = state[h * 128 : (h + 1) * 128, :]
        prefix_sum = jnp.sum(state_sum[h * 128 : (h + 1) * 128, :], axis=1, keepdims=True)
        linear = jnp.where(linear_mask, dot_wide(qf, kft), 0.0)
        linear_sum = dot_left(linear, vext) + dot_wide(qf, prefix)
        linear_total = jnp.sum(linear, axis=1, keepdims=True) + dot_wide(
            qf, jnp.broadcast_to(prefix_sum, (128, 128))
        )
        lift = jnp.exp(-window_best)
        inverse = 1.0 / (window_total + lift * linear_total)
        student = (window_sum + lift * linear_sum) * inverse
        difference = student - teacher[h * rows : (h + 1) * rows]
        square = difference * difference
        for k in range(rows // 8):
            loss = loss + square[k * 8 : (k + 1) * 8]
        grad_out = difference * (2.0 / tokens)
        num_grad = lift * grad_out * inverse
        den_grad = -lift * jnp.sum(grad_out * student, axis=1, keepdims=True) * inverse
        ngt = num_grad.T
        dgt = den_grad.T
        link = jnp.where(turned_mask, dot_right(vext, ngt) + dgt[:1], 0.0)
        qfg = dot_wide(kft, link) + dot_wide(prefix, ngt) + prefix_sum * dgt[:1]
        kfg_out[h * 128 : (h + 1) * 128] = dot_wide(qft, link, NT)
        adjoint = dot_wide(ngt, qft, NT)
        for k in range(4):
            x_out[4 * h + k, 0:32] = adjoint[32 * k : 32 * (k + 1)]
        rows_of_a.append(dot_wide(dgt[:8], qft, NT))
        grad_query = dot_left(features_back(qft, qfg), q)
        for k in range(4):
            x_out[4 * h + k, 40:56] = grad_query[16 * k : 16 * (k + 1)]
    tile_out[...] = loss
    pair = jnp.where(iota((8, 128), 0) == 0, rows_of_a[0], rows_of_a[1])
    for k in range(RING):
        x_out[k, 32:40] = pair


def attend(q, kb, vb, wq, wk):
    shape = jax.ShapeDtypeStruct
    big = pltpu.VMEM((256, 128), F32)
    return pl.pallas_call(
        attend_kernel,
        out_shape=(
            shape((RING, 56, 128), F32),
            shape((8, 128), F32),
            shape((256, 256), F32),
            shape((256, 256), F32),
            shape((256, 128), BF16),
            shape((256, 128), BF16),
        ),
        in_specs=[VMEM] * 5,
        out_specs=(VMEM,) * 6,
        scratch_shapes=[
            pltpu.VMEM((RING * RING // CHUNK, 256, CHUNK * 128), F32),
            big, big, big, big, big,
        ],
        name="attend",
    )(q, kb, vb, wq, wk)


def key_grad_kernel(x_ref, tile_ref, kf_ref, kfg_ref, kext_ref, vext_ref, out):
    z, y = lax.axis_index(Z), lax.axis_index(Y)
    me = z * RING + y
    at = iota((1, 256), 1)
    covered = (at >= WINDOW) & (at < WINDOW + 128) & (me * 128 - 128 + at >= 0)
    kext, vext = kext_ref[...], vext_ref[...]
    for h in range(2):
        later = x_ref[4 * h : 4 * h + 4, 0:32].reshape(128, 128)
        add = dot_right(vext, later) + x_ref[0, 32 + h : 33 + h]
        grad = kfg_ref[h * 128 : (h + 1) * 128] + add.T
        grad = jnp.where(covered, grad, 0.0)
        grad_key = dot_left(features_back(kf_ref[h * 128 : (h + 1) * 128], grad), kext)
        for k in range(4):
            out[4 * h + k, 0:16] = grad_key[16 * k : 16 * (k + 1)]
    for k in range(RING):
        out[k, 16:24] = tile_ref[...]


def key_grad(*args):
    return pl.pallas_call(
        key_grad_kernel,
        out_shape=jax.ShapeDtypeStruct((RING, 24, 128), F32),
        in_specs=[VMEM] * len(args),
        out_specs=VMEM,
        name="key_grad",
    )(*args)


def local(queries, keys, values, query_weight, key_weight):
    tokens = queries.shape[0] * RING * RING
    q = jnp.transpose(queries, (1, 0, 2))
    kb, vb = gather(keys, values)
    x, tile, kf, kfg, kext, vext = attend(q, kb, vb, query_weight, key_weight)
    sums, tile = exchange(x, 40, 1, tile)
    last = exchange(key_grad(sums, tile, kf, kfg, kext, vext), 0, 2)[0]
    grad_query = sums[:, 40:56].reshape(2, 64, 128)
    grad_key = last[:, 0:16].reshape(2, 64, 128)
    loss = (jnp.sum(last[0, 16:24]) / tokens).reshape(1)
    return loss, grad_query, grad_key


def solution(mesh):
    split = Mesh(
        mesh.devices.reshape(8, 8, mesh.shape["head"], mesh.shape["rep"]),
        (Z, Y, X, "rep"),
    )
    return jax.shard_map(
        local,
        mesh=split,
        in_specs=(
            P(REP_SEQ, X, None),
            P(REP_SEQ, None),
            P(REP_SEQ, None),
            P(("rep", X), None, None),
            P(("rep", X), None, None),
        ),
        out_specs=(P("rep"), P(("rep", X), None, None), P(("rep", X), None, None)),
        check_vma=False,
    )
```

time: 314 us -> 121 us (0.39)
  waiting for transfers between devices: 186 us -> 0 us
  Pallas kernels: 0 us -> 112 us
  starting transfers between devices: 39.3 us -> 0 us
  blocking collectives: 32.3 us -> 0 us
  matrix products: 20.4 us -> 0 us
  between operations: 14.7 us -> 2.44 us
  other arithmetic: 11.3 us -> 1.29 us
  local copies, waits for them, and re-layouts: 8.71 us -> 4.43 us
    all_gather x3 -> x0, waiting for transfers between devices: 128 us -> none  [the longest x1 81.6 us: in_one_piece(): lax.all_gather(both, axis, axis=dim, tiled=True)]
    pallas_call x0 -> x5, Pallas kernels: none -> 112 us  [the longest x2 56.5 us: exchange(): pl.pallas_call(functools.partial(exchange_kernel, scan, rows, tile is not...]
    all_to_all x6 -> x0, waiting for transfers between devices: 57.5 us -> none  [the longest x4 33.7 us: from_everyone(): lax.all_to_all(jnp.broadcast_to(x[None], (peers, *x.shape)), axis, 0, 0,...]
    all_gather x2 -> x0, blocking collectives: 32.3 us -> none  [entering(): pieces = jax.tree.map(lambda part: lax.all_gather(part, axis), total)]
    all_to_all x6 -> x0, starting transfers between devices: 32.2 us -> none  [the longest x4 23 us: from_everyone(): lax.all_to_all(jnp.broadcast_to(x[None], (peers, *x.shape)), axis, 0, 0,...]
    dot_general x18 -> x0, matrix products: 18.7 us -> none  [the longest x1 3.51 us: flash_update(): jnp.einsum('thd,jd->htj', queries, keys, preferred_element_type=jnp.float32)]
    ppermute x2 -> x0, starting transfers between devices: 6.94 us -> none  [shifted(): lax.ppermute(value, axis, [(source, source + steps) for source in range(l...]
    le x1 -> x0, other arithmetic: 3.72 us -> none  [flash_update(): allowed = (key_place[None, :] <= query_place[:, None])[None]]
  transfers between devices with their start and end apart: 11 -> 0, of which waited for: 7 -> 0; matrix products, arithmetic and copies ran while one was open for 10% -> 0% of each run, Pallas kernels for 0% -> 0%
where the time goes in v1:
time: 121 us
  Pallas kernels  112 us (93%)
  local copies, waits for them, and re-layouts  4.43 us (4%)
  between operations  2.44 us (2%)
  other arithmetic  1.29 us (1%)
    pallas_call x2, Pallas kernels, exchange(): pl.pallas_call(functools.partial(exchange_kernel, scan, rows, tile is not...  56.5 us
    pallas_call x1, Pallas kernels, gather(): pl.pallas_call(gather_kernel, out_shape=(blocks, blocks), in_specs=[VMEM]...  46.4 us
    pallas_call x1, Pallas kernels, attend(): pl.pallas_call(attend_kernel, out_shape=(shape((RING, 56, 128), F32), sha...  6.93 us
    pallas_call x1, Pallas kernels, key_grad(): pl.pallas_call(key_grad_kernel, out_shape=jax.ShapeDtypeStruct((RING, 24,...  2.56 us

profile of v1, /device:TPU:6, one launch (start us, length us, event | category | flops | bytes accessed | tf_op | source)
XLA Modules:
  0.0 120.5 jit_solution(7225668623545456404)
XLA Ops:
  0.6 1.5 %copy.10 = bf16[128,2,128]{2,0,1:T(8,128)(2,1)} copy(bf16[128,2,128]{2,1,0:T(2,128)(2,1)} %param.5) | data formatting | bytes 131072 | tf_op args[0]
  2.1 46.4 %gather_kv.1 = (bf16[64,128,128]{2,1,0:T(8,128)(2,1)}, bf16[64,128,128]{2,1,0:T(8,128)(2,1)}) custom-call(bf16[128,128]{1,0:T(8,128)(2,1)} %k_ref.1, bf16[128,128]{1,0:T(8,128)(2,1)} %v_ref.1), custom_call_target="tpu_custom_call" | custom-call | tf_op jit(solution)/shard_map/gather_kv/pallas_call | solution.py:104
  48.5 6.9 %attend.1 = (f32[8,56,128]{2,1,0:T(8,128)}, f32[8,128]{1,0:T(8,128)}, f32[256,256]{1,0:T(8,128)}, f32[256,256]{1,0:T(8,128)}, bf16[256,128]{1,0:T(8,128)(2,1)}, /*index=5*/bf16[256,128]{1,0:T(8,128)(2,1)}) custom-call(bf16[2,128,128]{2,1,0:T(8,128)(2,1)} %bitcast.6, bf16[64,128,128]{2,1,0:T(8,128)(2,1)} %get-tuple-element.13.kb, ...), custom_call_target="tpu_custom_call" | custom-call | tf_op jit(solution)/shard_map/attend/pallas_call | solution.py:390
  55.5 34.9 %exchange.2 = (f32[8,56,128]{2,1,0:T(8,128)}, f32[8,128]{1,0:T(8,128)}) custom-call(f32[8,56,128]{2,1,0:T(8,128)} %get-tuple-element.15.refs_0_, f32[8,128]{1,0:T(8,128)} %get-tuple-element.16.refs_1_), custom_call_target="tpu_custom_call" | custom-call | tf_op jit(solution)/shard_map/exchange/pallas_call | solution.py:197
  90.3 2.6 %key_grad.1.refs_0_ = f32[8,24,128]{2,1,0:T(8,128)} custom-call(f32[8,56,128]{2,1,0:T(8,128)} %get-tuple-element.17.x_ref, f32[8,128]{1,0:T(8,128)} %get-tuple-element.18.tile_ref, f32[256,256]{1,0:T(8,128)} %get-tuple-element.19.kf_ref, f32[256,256]{1,0:T(8,128)} %get-tuple-element.20.kfg_ref, bf16[256,128]{1,0:T(8,128)(2,1)} %get-tuple-element.21.kext_ref, ...), custom_call_target="tpu_custom_call" | custom-call | tf_op jit(solution)/shard_map/key_grad/pallas_call | solution.py:429
  92.9 1.5 %slice.10 = f32[8,16,128]{2,1,0:T(8,128)} slice(f32[8,56,128]{2,1,0:T(8,128)} %get-tuple-element.17.x_ref), slice={[0:8], [40:56], [0:128]} | slice | bytes 131072 | tf_op jit(solution)/shard_map/slice | solution.py:445
  94.4 21.6 %exchange.3 = f32[8,24,128]{2,1,0:T(8,128)} custom-call(f32[8,24,128]{2,1,0:T(8,128)} %key_grad.1.refs_0_), custom_call_target="tpu_custom_call" | custom-call | tf_op jit(solution)/shard_map/exchange/pallas_call | solution.py:197
  116.0 1.3 %slice_reduce_fusion = f32[]{:T(128)} fusion(f32[8,24,128]{2,1,0:T(8,128)} %exchange.3), kind=kLoop, calls=%fused_computation.1 | loop fusion | flops 1023 | bytes 4100 | tf_op jit(solution)/shard_map/reduce_sum | solution.py:447
  117.9 1.5 %slice.11 = f32[8,16,128]{2,1,0:T(8,128)} slice(f32[8,24,128]{2,1,0:T(8,128)} %exchange.3), slice={[0:8], [0:16], [0:128]} | slice | bytes 131072 | tf_op jit(solution)/shard_map/slice | solution.py:446

commit v2 on v1

v2 whole, which is shorter than its diff:
```python
import functools

import jax
import jax.numpy as jnp
from jax import lax
from jax.experimental import pallas as pl
from jax.experimental.pallas import tpu as pltpu
from jax.sharding import Mesh
from jax.sharding import PartitionSpec as P

WINDOW = 64
Z, Y, X = "seq_0", "seq_1", "head"
REP_SEQ = ("rep", Z, Y)
MESH = pl.DeviceIdType.MESH
RING = 8
LOW = -1e30
F32 = jnp.float32
BF16 = jnp.bfloat16
FAR_FIRST = (4, 3, 5, 2, 6, 1, 7)


def around(place, steps):
    return lax.rem(place + (steps + RING), RING)


def remote(src, dst, send, recv, axis, place):
    return pltpu.make_async_remote_copy(
        src_ref=src,
        dst_ref=dst,
        send_sem=send,
        recv_sem=recv,
        device_id={axis: place},
        device_id_type=MESH,
    )


def greet(peers):
    barrier = pltpu.get_barrier_semaphore()
    for axis, place in peers:
        pl.semaphore_signal(barrier, inc=1, device_id={axis: place}, device_id_type=MESH)
    pl.semaphore_wait(barrier, len(peers))


NN = (((1,), (0,)), ((), ()))
NT = (((1,), (1,)), ((), ()))


def dot(a, b, dims=NN):
    return lax.dot_general(a, b, dims, preferred_element_type=F32)


def two(a):
    high = a.astype(BF16)
    return high, (a - high.astype(F32)).astype(BF16)


def dot_wide(a, b, dims=NN):
    a_high, a_low = two(a)
    b_high, b_low = two(b)
    return dot(a_high, b_high, dims) + (dot(a_high, b_low, dims) + dot(a_low, b_high, dims))


def dot_left(a, b, dims=NN):
    high, low = two(a)
    return dot(high, b, dims) + dot(low, b, dims)


def dot_right(a, b, dims=NN):
    high, low = two(b)
    return dot(a, high, dims) + dot(a, low, dims)


def three(a):
    high = a.astype(BF16)
    rest = a - high.astype(F32)
    mid = rest.astype(BF16)
    return high, mid, (rest - mid.astype(F32)).astype(BF16)


def features_of(pieces, tokens):
    act = dot(pieces[0], tokens, NT) + (dot(pieces[1], tokens, NT) + dot(pieces[2], tokens, NT))
    half = 64
    parts = []
    for h in range(act.shape[0] // half):
        one = act[h * half : (h + 1) * half]
        for e in (jnp.exp(one), jnp.exp(-one)):
            parts.append(e * (1.0 / jnp.sum(e, axis=0, keepdims=True)))
    return jnp.concatenate(parts, axis=0)


def features_back(features, grad):
    half = features.shape[0] // 2
    p, r = features[:half], features[half:]
    dp, dr = grad[:half], grad[half:]
    return p * (dp - jnp.sum(p * dp, axis=0, keepdims=True)) - r * (
        dr - jnp.sum(r * dr, axis=0, keepdims=True)
    )


def iota(shape, axis):
    return lax.broadcasted_iota(jnp.int32, shape, axis)


NEAR_FIRST = (1, 7, 2, 6, 3, 5, 4)
ROWS = 128
HALF = 64
TOKENS = ROWS * RING * RING
LINE = RING * HALF


def layer_kernel(
    q_ref, k_ref, v_ref, wq_ref, wk_ref,
    out_g, out_k, out_loss,
    kbuf, vbuf, scores, f_high, f_low, best, state, state_sum, total, accum,
    krow, vrow, e_row, kag, arows, acol,
    x, b1, t1, b2, suffix, g, g1, g1s, g2, g2s, tile, tiles, tile_x, l1, l1s, l2, gp, ba, bas, bb, bbs,
    kv_send, k_recv, v_recv, send, recv,
):
    z, y, xx = lax.axis_index(Z), lax.axis_index(Y), lax.axis_index(X)
    me = z * RING + y
    place = {Z: z, Y: y}
    others = [lax.rem(xx + d, 4) for d in (2, 1, 3)]
    near = [(axis, around(place[axis], d)) for axis in (Z, Y) for d in (1, -1)]
    greet(near + [(X, p) for p in others])

    k_streams = ((kbuf, kv_send.at[0], k_recv, 0, Y, Z), (kbuf, kv_send.at[1], k_recv, 1, Z, Y))
    v_streams = ((vbuf, kv_send.at[2], v_recv, 0, Y, Z), (vbuf, kv_send.at[3], v_recv, 1, Z, Y))

    def piece(stream, along, across):
        line = around(place[stream[5]], across)
        return (stream[3] * RING + line) * RING + around(place[stream[4]], along)

    def push(stream, src, at, axis, step):
        to = around(place[axis], step)
        remote(src, stream[0].at[at], stream[1], stream[2].at[at], axis, to).start()

    def forward(stream, at, axis, step):
        push(stream, stream[0].at[at], at, axis, step)

    def arrived(stream, at):
        block = stream[0].at[at]
        remote(block, block, stream[1], stream[2].at[at], Z, z).wait_recv()

    halves = (pl.ds(0, HALF), pl.ds(HALF, HALF))
    for stream in k_streams:
        at, src = piece(stream, 0, 0), k_ref.at[halves[stream[3]]]
        for axis in (stream[4], stream[5]):
            for way in (1, -1):
                push(stream, src, at, axis, way)
    for stream in v_streams:
        at, src = piece(stream, 0, 0), v_ref.at[halves[stream[3]]]
        for way in (1, -1):
            push(stream, src, at, stream[4], way)

    for ref, streams in ((k_ref, k_streams), (v_ref, v_streams)):
        for stream in streams:
            stream[0][piece(stream, 0, 0)] = ref[halves[stream[3]]]
    best[...] = jnp.full(best.shape, LOW, F32)
    for ref in (state, state_sum, total, accum):
        ref[...] = jnp.zeros_like(ref)
    queries = [q_ref[:, h, :] for h in range(2)]
    q_all = jnp.concatenate(queries, axis=0)
    wk = three(wk_ref[...].reshape(2 * HALF, 128))

    for hop in range(1, 5):
        for way in (1, -1):
            if hop == 4 and way == -1:
                continue
            for stream in k_streams + v_streams:
                at = piece(stream, -way * hop, 0)
                arrived(stream, at)
                if hop < (4 if way == 1 else 3):
                    forward(stream, at, stream[4], way)
                if stream[0] is kbuf:
                    forward(stream, at, stream[5], 1)
                    forward(stream, at, stream[5], -1)

    def pass_on(streams, hop):
        for along in (0, -1, 1, -2, 2, -3, 3, 4):
            for way in (1, -1):
                last = (way == 1) == (along % 2 == 0)
                if hop == 4 and not last:
                    continue
                for stream in streams:
                    at = piece(stream, along, -way * hop)
                    arrived(stream, at)
                    if hop < 3 or (hop == 3 and last):
                        forward(stream, at, stream[5], way)

    first = me * ROWS
    bound = first - WINDOW
    scale = 128 ** (-0.5)
    lane = iota((1, LINE), 1)
    lane_block, lane_row = jnp.right_shift(lane, 6), jnp.bitwise_and(lane, HALF - 1)
    query_place = first + jnp.bitwise_and(iota((2 * ROWS, 1), 0), ROWS - 1)

    def lanes(fold, start, value):
        for k in range(LINE // 128):
            start = fold(start, value[:, k * 128 : (k + 1) * 128])
        return start

    def on_keys(c):
        line = jnp.bitwise_and(c, RING - 1)
        second = c >= RING
        at = jnp.where(second, line * ROWS + HALF, line * (ROWS * RING))
        at = at + lane_block * jnp.where(second, ROWS * RING, ROWS) + lane_row
        kc = kbuf[pl.ds(c * RING, RING)].reshape(LINE, 128)
        s = dot(q_all, kc, NT) * scale
        s = jnp.where(at <= query_place, s, LOW)
        scores[c] = s
        best[...] = lanes(jnp.maximum, best[...], s)
        f = jnp.where(at < bound, features_of(wk, kc), 0.0)
        state_sum[...] = lanes(jnp.add, state_sum[...], f)
        f_high[c], f_low[c] = two(f)

    def on_values(top, c):
        vc = vbuf[pl.ds(c * RING, RING)].reshape(LINE, 128)
        w = jnp.exp(scores[c] - top)
        total[...] = lanes(jnp.add, total[...], w)
        accum[...] += dot(w.astype(BF16), vc)
        state[...] += dot(f_high[c], vc) + dot(f_low[c], vc)

    def lines(hop, work):
        @pl.loop(0, 4 if 0 < hop < 4 else 2)
        def _(i):
            second = jnp.bitwise_and(i, 1)
            steps = jnp.where(i < 2, RING - hop, RING + hop)
            c = second * RING + lax.rem(jnp.where(second == 1, y, z) + steps, RING)

            @pl.when(jnp.logical_or(second == 1, c <= z))
            def _():
                work(c)

    lines(0, on_keys)
    for hop in range(1, 5):
        pass_on(k_streams, hop)
        if hop == 3:
            for stream in v_streams:
                for along in (0, -1, 1, -2, 2, -3, 3, 4):
                    at = piece(stream, along, 0)
                    for way in (1, -1):
                        forward(stream, at, stream[5], way)
        lines(hop, on_keys)
    top = jnp.max(best[...], axis=1, keepdims=True)
    on_values = functools.partial(on_values, top)
    lines(0, on_values)

    before = jnp.where(y > 0, (RING + y - 1) * RING + z, (2 * RING - 1) * RING + jnp.maximum(z - 1, 0))
    tt, jj = iota((ROWS, 2 * ROWS), 0), iota((ROWS, 2 * ROWS), 1)
    window = (jj > tt) & (jj <= tt + WINDOW) & (bound + jj >= 0)
    tt, jj = iota((ROWS, ROWS), 0), iota((ROWS, ROWS), 1)
    linear_mask = (jj <= tt) & (bound + jj >= 0)
    turned_mask = (tt <= jj) & (bound + tt >= 0)
    kext = jnp.concatenate([kbuf[before], k_ref[...], k_ref[pl.ds(HALF, HALF)]], axis=0)
    kf_all = features_of(wk, kext[:ROWS])
    heads = []
    for h in range(2):
        q = queries[h]
        s = dot(q, kext, NT) * scale
        window_best = jnp.max(jnp.where(window, s, LOW), axis=1, keepdims=True)
        weights = jnp.where(window, jnp.exp(s - window_best), 0.0)
        window_total = jnp.sum(weights, axis=1, keepdims=True)
        qft = features_of(three(wq_ref[h]), q)
        qf = qft.T
        kft = kf_all[h * ROWS : (h + 1) * ROWS]
        linear = jnp.where(linear_mask, dot_wide(qf, kft), 0.0)
        prefix_sum = jnp.sum(state_sum[h * ROWS : (h + 1) * ROWS, :], axis=1, keepdims=True)
        linear_total = jnp.sum(linear, axis=1, keepdims=True) + dot_wide(
            qf, jnp.broadcast_to(prefix_sum, (128, 128))
        )
        lift = jnp.exp(-window_best)
        inverse = 1.0 / (window_total + lift * linear_total)
        heads.append((q, weights.astype(BF16), qft, qf, kft, linear, prefix_sum, lift, inverse))

    for hop in range(1, 5):
        pass_on(v_streams, hop)
        lines(hop, on_values)

    vext = jnp.concatenate([vbuf[before], v_ref[...], v_ref[pl.ds(HALF, HALF)]], axis=0)
    teacher = accum[...] / jnp.sum(total[...], axis=1, keepdims=True)
    teacher = teacher.astype(BF16).astype(F32)
    loss = jnp.zeros((8, 128), F32)
    kept = []
    for h in range(2):
        q, weights, qft, qf, kft, linear, prefix_sum, lift, inverse = heads[h]
        prefix = state[h * ROWS : (h + 1) * ROWS, :]
        window_sum = dot(weights, vext)
        linear_sum = dot_left(linear, vext[:ROWS]) + dot_wide(qf, prefix)
        student = (window_sum + lift * linear_sum) * inverse
        difference = student - teacher[h * ROWS : (h + 1) * ROWS]
        square = difference * difference
        for k in range(ROWS // 8):
            loss = loss + square[k * 8 : (k + 1) * 8]
        grad_out = difference * (2.0 / TOKENS)
        num_grad = lift * grad_out * inverse
        den_grad = -lift * jnp.sum(grad_out * student, axis=1, keepdims=True) * inverse
        dgt = den_grad.T
        adjoint = dot_wide(qft, num_grad)
        a_row = dot_wide(jnp.broadcast_to(dgt[:1], (8, ROWS)), qft, NT)
        for k in range(4):
            x[4 * h + k, 0:32] = adjoint[32 * k : 32 * (k + 1)]
            x[4 * h + k, 32:33] = a_row[:1]
        kept.append((prefix, num_grad, dgt))

    def start(k, axis, src, dst):
        for d in FAR_FIRST:
            p = around(place[axis], d)
            remote(src(p), dst.at[place[axis]], send.at[k], recv.at[k, place[axis]], axis, p).start()

    def finish(k, axis, dst):
        for d in NEAR_FIRST:
            p = around(place[axis], d)
            remote(dst.at[p], dst.at[p], send.at[k], recv.at[k, p], axis, p).wait_recv()

    def added(ref, low=0, high=RING):
        out = ref[low]
        for k in range(low + 1, high):
            out = out + ref[k]
        return out

    start(0, Y, lambda p: x.at[p], b1)
    b1[y] = x[y]
    tile[...] = loss
    for p in others:
        remote(tile, tiles.at[xx], send.at[1], recv.at[1, xx], X, p).start()
    tiles[xx] = loss

    for h in range(2):
        q, weights, qft, qf, kft, linear, prefix_sum, lift, inverse = heads[h]
        prefix, num_grad, dgt = kept[h]
        ngt = num_grad.T
        link = jnp.where(turned_mask, dot_right(vext[:ROWS], ngt) + dgt[:1], 0.0)
        qfg = dot_wide(kft, link) + dot_wide(prefix, ngt) + prefix_sum * dgt[:1]
        kfg = dot_wide(qft, link, NT)
        grad_query = dot_left(features_back(qft, qfg), q)
        grad_key = dot_left(features_back(kft, kfg), kext[:ROWS])
        for k in range(4):
            g[4 * h + k, 0:16] = grad_query[16 * k : 16 * (k + 1)]
            g[4 * h + k, 16:32] = grad_key[16 * k : 16 * (k + 1)]
    start(2, Z, lambda p: g.at[p], g1)
    g1[z] = g[z]

    own_head, part = jnp.right_shift(y, 2), jnp.bitwise_and(y, 3)
    sign = jnp.where(part < 2, 1.0, -1.0).astype(F32)
    within = pl.multiple_of(jnp.bitwise_and(part, 1) * 32, 32)
    for k in range(RING):
        if k:
            at = (RING + k - 1) * RING + z
        else:
            at = (2 * RING - 1) * RING + jnp.maximum(z - 1, 0)
        for row, buf in ((krow, kbuf), (vrow, vbuf)):
            row[k, 0:HALF] = buf[at]
            row[k, HALF:ROWS] = buf[z * RING + k]
    keys_row = krow[...].reshape(RING * ROWS, 128)
    pieces = three(wk_ref[own_head])
    act = dot(pieces[0], keys_row, NT) + (dot(pieces[1], keys_row, NT) + dot(pieces[2], keys_row, NT))
    e = jnp.exp(act * sign)
    e_row[...] = e * (1.0 / jnp.sum(e, axis=0, keepdims=True))

    finish(0, Y, b1)
    t1[...] = added(b1)
    start(3, Z, lambda p: t1, b2)
    for p in others:
        remote(tile, tiles.at[p], send.at[1], recv.at[1, p], X, p).wait_recv()
    tile_x[...] = added(tiles, 0, 4)
    start(4, Z, lambda p: tile_x, l1)
    l1[z] = tile_x[...]
    finish(2, Z, g1)
    g1s[...] = added(g1)
    start(5, Y, lambda p: g1s, g2)
    g2[y] = g1s[...]
    b2[z] = t1[...]
    finish(3, Z, b2)

    base = jnp.zeros((33, 128), F32)
    for k in range(1, RING):
        base = base + jnp.where(k > z, b2[k], 0.0)
    for k in reversed(range(RING)):
        suffix[k] = base
        arows[k : k + 1, :] = base[32:33]
        base = base + b1[k]
    acol[...] = arows[...].T
    columns = acol[pl.ds(pl.multiple_of(part * 32, 32), 32), :]
    grads = []
    for k in range(RING):
        grads.append(dot_left(suffix[k, 0:32], vrow[k], NT) + columns[:, k : k + 1])
    weighted = jnp.concatenate(grads, axis=1) * e_row[pl.ds(within, 32), :]
    kag[...] = -e_row[...] * jnp.sum(weighted, axis=0, keepdims=True)
    kag[pl.ds(within, 32), :] += weighted
    real = (iota((1, RING * ROWS), 1) >= HALF) | (z > 0)
    far = dot_left(jnp.where(real, kag[...] * sign, 0.0), keys_row)
    for k in range(RING):
        gp[k] = far[8 * k : 8 * (k + 1)]
    start(6, Z, lambda p: gp.at[p], ba)
    ba[z] = gp[z]

    finish(5, Y, g2)
    g2s[...] = added(g2)
    start(7, Z, lambda p: g2s, out_g)
    out_g[z] = g2s[...]
    finish(4, Z, l1)
    l1s[...] = added(l1)
    start(8, Y, lambda p: l1s, l2)
    l2[y] = l1s[...]

    finish(6, Z, ba)
    bas[...] = added(ba)
    start(9, Y, lambda p: bas, bb)
    bb[y] = bas[...]
    finish(9, Y, bb)
    bbs[0:8] = added(bb, 0, 4)
    bbs[8:16] = added(bb, 4, 8)
    start(10, Z, lambda p: bbs, out_k)
    out_k[z] = bbs[...]
    finish(8, Y, l2)
    out_loss[...] = added(l2)
    finish(7, Z, out_g)
    finish(10, Z, out_k)

    for stream in k_streams + v_streams:
        sent = stream[0].at[pl.ds(0, RING * RING - 1)]
        remote(sent, sent, stream[1], stream[2].at[0], Z, z).wait_send()
    for k, ref, count in (
        (0, b1, 7), (1, tiles, 3), (2, g1, 7), (3, b2, 7), (4, l1, 7), (5, g2, 7),
        (6, ba, 7), (7, out_g, 7), (8, l2, 7), (9, bb, 7), (10, out_k, 7),
    ):
        sent = ref.at[pl.ds(0, count)]
        remote(sent, sent, send.at[k], recv.at[k, 0], Z, z).wait_send()


VMEM = pl.BlockSpec(memory_space=pltpu.VMEM)


def layer(queries, keys, values, query_weight, key_weight):
    shape = jax.ShapeDtypeStruct
    dma = pltpu.SemaphoreType.DMA

    def f32(*dims):
        return pltpu.VMEM(dims, F32)

    def bf16(*dims):
        return pltpu.VMEM(dims, BF16)

    blocks = bf16(2 * RING * RING, HALF, 128)
    scratch = [
        blocks, blocks, f32(16, 256, LINE), bf16(16, 256, LINE), bf16(16, 256, LINE),
        f32(256, 128), f32(256, 128), f32(256, 128), f32(256, 128), f32(256, 128),
        bf16(8, 128, 128), bf16(8, 128, 128), f32(64, 1024), f32(64, 1024), f32(8, 128), f32(128, 8),
        f32(8, 33, 128), f32(8, 33, 128), f32(33, 128), f32(8, 33, 128), f32(8, 33, 128),
        f32(8, 32, 128), f32(8, 32, 128), f32(32, 128), f32(8, 32, 128), f32(32, 128),
        f32(8, 128), f32(4, 8, 128), f32(8, 128), f32(8, 8, 128), f32(8, 128), f32(8, 8, 128),
        f32(8, 8, 128), f32(8, 8, 128), f32(8, 128), f32(8, 8, 128), f32(16, 128),
        dma((4,)), dma((128,)), dma((128,)), dma((11,)), dma((11, RING)),
    ]
    return pl.pallas_call(
        layer_kernel,
        out_shape=(shape((8, 32, 128), F32), shape((8, 16, 128), F32), shape((8, 128), F32)),
        in_specs=[VMEM] * 5,
        out_specs=(VMEM,) * 3,
        scratch_shapes=scratch,
        compiler_params=pltpu.CompilerParams(
            collective_id=0, has_side_effects=True, vmem_limit_bytes=60 * 1024 * 1024
        ),
        name="layer",
    )(queries, keys, values, query_weight, key_weight)


def finish_kernel(g_ref, k_ref, loss_ref, loss, grad_query, grad_key):
    loss[0] = jnp.sum(loss_ref[...]) * (1.0 / TOKENS)
    grad_query[...] = g_ref[:, 0:16].reshape(2, HALF, 128)
    near = g_ref[:, 16:32].reshape(2, HALF, 128)
    for h in range(2):
        grad_key[h] = near[h] + k_ref[:, 8 * h : 8 * (h + 1)].reshape(HALF, 128)


def local(queries, keys, values, query_weight, key_weight):
    shape = jax.ShapeDtypeStruct
    return pl.pallas_call(
        finish_kernel,
        out_shape=(
            shape((1,), F32), shape(query_weight.shape, F32), shape(key_weight.shape, F32)
        ),
        in_specs=[VMEM] * 3,
        out_specs=(pl.BlockSpec(memory_space=pltpu.SMEM), VMEM, VMEM),
        name="finish",
    )(*layer(queries, keys, values, query_weight, key_weight))


def solution(mesh):
    split = Mesh(
        mesh.devices.reshape(8, 8, mesh.shape["head"], mesh.shape["rep"]),
        (Z, Y, X, "rep"),
    )
    return jax.shard_map(
        local,
        mesh=split,
        in_specs=(
            P(REP_SEQ, X, None),
            P(REP_SEQ, None),
            P(REP_SEQ, None),
            P(("rep", X), None, None),
            P(("rep", X), None, None),
        ),
        out_specs=(P("rep"), P(("rep", X), None, None), P(("rep", X), None, None)),
        check_vma=False,
    )
```

time: 121 us -> 86.9 us (0.72)
  Pallas kernels: 112 us -> 85 us
  local copies, waits for them, and re-layouts: 4.43 us -> 0 us
  between operations: 2.44 us -> 0.64 us
  other arithmetic: 1.29 us -> 0 us
    pallas_call x5 -> x2, Pallas kernels: 112 us -> 85 us  [the longest x1 83.3 us: layer(): pl.pallas_call(layer_kernel, out_shape=(shape((8, 32, 128), F32), shape((...]
    slice x2 -> x0, local copies, waits for them, and re-layouts: 2.95 us -> none  [the longest x1 1.48 us: local(): grad_key = last[:, 0:16].reshape(2, 64, 128)]
    unnamed x1 -> x0, local copies, waits for them, and re-layouts: 1.48 us -> none
    reduce_sum x1 -> x0, other arithmetic: 1.29 us -> none  [local(): loss = (jnp.sum(last[0, 16:24]) / tokens).reshape(1)]
where the time goes in v2:
time: 86.9 us; the launch traced here: 85.6 us
  Pallas kernels  85 us (98%)
    pallas_call x1, Pallas kernels, layer(): pl.pallas_call(layer_kernel, out_shape=(shape((8, 32, 128), F32), shape((...  83.3 us

profile of v2, /device:TPU:6, one launch (start us, length us, event | category | flops | bytes accessed | tf_op | source)
XLA Modules:
  0.0 85.6 jit_solution(11219358879097419901)
XLA Ops:
  0.6 83.3 %layer.1 = (f32[8,32,128]{2,1,0:T(8,128)}, f32[8,16,128]{2,1,0:T(8,128)}, f32[8,128]{1,0:T(8,128)}) custom-call(bf16[128,2,128]{2,1,0:T(2,128)(2,1)} %q_ref.1, bf16[128,128]{1,0:T(8,128)(2,1)} %k_ref.1, bf16[128,128]{1,0:T(8,128)(2,1)} %v_ref.1, f32[2,64,128]{2,1,0:T(8,128)} %wq_ref.1, f32[2,64,128]{2,1,0:T(8,128)} %wk_ref.1), custom_call_target="tpu_custom_call" | custom-call | tf_op jit(solution)/shard_map/layer/pallas_call | solution.py:455
  84.0 1.6 %finish.1 = (f32[1]{0:T(128)}, f32[2,64,128]{2,1,0:T(8,128)}, f32[2,64,128]{2,1,0:T(8,128)}) custom-call(f32[8,32,128]{2,1,0:T(8,128)} %get-tuple-element.6.g_ref, f32[8,16,128]{2,1,0:T(8,128)} %get-tuple-element.7.k_ref, f32[8,128]{1,0:T(8,128)} %get-tuple-element.8.loss_ref), custom_call_target="tpu_custom_call" | custom-call | tf_op jit(solution)/shard_map/finish/pallas_call | solution.py:478

commit v3 on v2

--- a/solution.py
+++ b/solution.py
@@ -120,8 +120,7 @@
     me = z * RING + y
     place = {Z: z, Y: y}
     others = [lax.rem(xx + d, 4) for d in (2, 1, 3)]
-    near = [(axis, around(place[axis], d)) for axis in (Z, Y) for d in (1, -1)]
-    greet(near + [(X, p) for p in others])
+    greet([(axis, around(place[axis], d)) for d in FAR_FIRST for axis in (Z, Y)] + [(X, p) for p in others])
 
     k_streams = ((kbuf, kv_send.at[0], k_recv, 0, Y, Z), (kbuf, kv_send.at[1], k_recv, 1, Z, Y))
     v_streams = ((vbuf, kv_send.at[2], v_recv, 0, Y, Z), (vbuf, kv_send.at[3], v_recv, 1, Z, Y))
@@ -144,13 +143,16 @@
     halves = (pl.ds(0, HALF), pl.ds(HALF, HALF))
     for stream in k_streams:
         at, src = piece(stream, 0, 0), k_ref.at[halves[stream[3]]]
-        for axis in (stream[4], stream[5]):
-            for way in (1, -1):
-                push(stream, src, at, axis, way)
+        for way in (1, -1):
+            push(stream, src, at, stream[5], way)
+    for ref, streams in ((k_ref, k_streams), (v_ref, v_streams)):
+        for step in (1, 7, 4, 3, 5, 2, 6):
+            for stream in streams:
+                push(stream, ref.at[halves[stream[3]]], piece(stream, 0, 0), stream[4], step)
     for stream in v_streams:
         at, src = piece(stream, 0, 0), v_ref.at[halves[stream[3]]]
         for way in (1, -1):
-            push(stream, src, at, stream[4], way)
+            push(stream, src, at, stream[5], way)
 
     for ref, streams in ((k_ref, k_streams), (v_ref, v_streams)):
         for stream in streams:
@@ -162,18 +164,13 @@
     q_all = jnp.concatenate(queries, axis=0)
     wk = three(wk_ref[...].reshape(2 * HALF, 128))
 
-    for hop in range(1, 5):
-        for way in (1, -1):
-            if hop == 4 and way == -1:
-                continue
-            for stream in k_streams + v_streams:
-                at = piece(stream, -way * hop, 0)
+    for streams in (k_streams, v_streams):
+        for along in NEAR_FIRST:
+            for stream in streams:
+                at = piece(stream, along, 0)
                 arrived(stream, at)
-                if hop < (4 if way == 1 else 3):
-                    forward(stream, at, stream[4], way)
-                if stream[0] is kbuf:
-                    forward(stream, at, stream[5], 1)
-                    forward(stream, at, stream[5], -1)
+                forward(stream, at, stream[5], 1)
+                forward(stream, at, stream[5], -1)
 
     def pass_on(streams, hop):
         for along in (0, -1, 1, -2, 2, -3, 3, 4):
@@ -234,16 +231,11 @@
     lines(0, on_keys)
     for hop in range(1, 5):
         pass_on(k_streams, hop)
-        if hop == 3:
-            for stream in v_streams:
-                for along in (0, -1, 1, -2, 2, -3, 3, 4):
-                    at = piece(stream, along, 0)
-                    for way in (1, -1):
-                        forward(stream, at, stream[5], way)
         lines(hop, on_keys)
+        if hop < 4:
+            pass_on(v_streams, hop)
     top = jnp.max(best[...], axis=1, keepdims=True)
     on_values = functools.partial(on_values, top)
-    lines(0, on_values)
 
     before = jnp.where(y > 0, (RING + y - 1) * RING + z, (2 * RING - 1) * RING + jnp.maximum(z - 1, 0))
     tt, jj = iota((ROWS, 2 * ROWS), 0), iota((ROWS, 2 * ROWS), 1)
@@ -272,9 +264,10 @@
         inverse = 1.0 / (window_total + lift * linear_total)
         heads.append((q, weights.astype(BF16), qft, qf, kft, linear, prefix_sum, lift, inverse))
 
-    for hop in range(1, 5):
-        pass_on(v_streams, hop)
+    for hop in range(4):
         lines(hop, on_values)
+    pass_on(v_streams, 4)
+    lines(4, on_values)
 
     vext = jnp.concatenate([vbuf[before], v_ref[...], v_ref[pl.ds(HALF, HALF)]], axis=0)
     teacher = accum[...] / jnp.sum(total[...], axis=1, keepdims=True)

time: 86.9 us -> 80.5 us (0.926); the launches traced: 85.6 us -> 80.2 us
  Pallas kernels: 85 us -> 79.6 us
    pallas_call x1, Pallas kernels: 83.3 us -> 77.9 us  [layer(): pl.pallas_call(layer_kernel, out_shape=(shape((8, 32, 128), F32), shape((...]
where the time goes in v3:
time: 80.5 us; the launch traced here: 80.2 us
  Pallas kernels  79.6 us (99%)
    pallas_call x1, Pallas kernels, layer(): pl.pallas_call(layer_kernel, out_shape=(shape((8, 32, 128), F32), shape((...  77.9 us
    pallas_call x1, Pallas kernels, local(): pl.pallas_call(finish_kernel, out_shape=(shape((1,), F32), shape(query_we...  1.61 us

profile of v3, /device:TPU:6, one launch (start us, length us, event | category | flops | bytes accessed | tf_op | source)
XLA Modules:
  0.0 80.2 jit_solution(7433921813089116167)
XLA Ops:
  0.6 77.9 %layer.1 = (f32[8,32,128]{2,1,0:T(8,128)}, f32[8,16,128]{2,1,0:T(8,128)}, f32[8,128]{1,0:T(8,128)}) custom-call(bf16[128,2,128]{2,1,0:T(2,128)(2,1)} %q_ref.1, bf16[128,128]{1,0:T(8,128)(2,1)} %k_ref.1, bf16[128,128]{1,0:T(8,128)(2,1)} %v_ref.1, f32[2,64,128]{2,1,0:T(8,128)} %wq_ref.1, f32[2,64,128]{2,1,0:T(8,128)} %wk_ref.1), custom_call_target="tpu_custom_call" | custom-call | tf_op jit(solution)/shard_map/layer/pallas_call | solution.py:448
  78.6 1.6 %finish.1 = (f32[1]{0:T(128)}, f32[2,64,128]{2,1,0:T(8,128)}, f32[2,64,128]{2,1,0:T(8,128)}) custom-call(f32[8,32,128]{2,1,0:T(8,128)} %get-tuple-element.6.g_ref, f32[8,16,128]{2,1,0:T(8,128)} %get-tuple-element.7.k_ref, f32[8,128]{1,0:T(8,128)} %get-tuple-element.8.loss_ref), custom_call_target="tpu_custom_call" | custom-call | tf_op jit(solution)/shard_map/finish/pallas_call | solution.py:471

commit v4 on v3

--- a/solution.py
+++ b/solution.py
@@ -112,8 +112,7 @@
     q_ref, k_ref, v_ref, wq_ref, wk_ref,
     out_g, out_k, out_loss,
     kbuf, vbuf, scores, f_high, f_low, best, state, state_sum, total, accum,
-    krow, vrow, e_row, kag, arows, acol,
-    x, b1, t1, b2, suffix, g, g1, g1s, g2, g2s, tile, tiles, tile_x, l1, l1s, l2, gp, ba, bas, bb, bbs,
+    far, g, g1, g1s, g2, g2s, tile, tiles, tile_x, l1, l1s, l2, gk, k1, k1s, k2, k2s,
     kv_send, k_recv, v_recv, send, recv,
 ):
     z, y, xx = lax.axis_index(Z), lax.axis_index(Y), lax.axis_index(X)
@@ -210,12 +209,23 @@
         state_sum[...] = lanes(jnp.add, state_sum[...], f)
         f_high[c], f_low[c] = two(f)
 
-    def on_values(top, c):
+    def on_state(c):
+        vc = vbuf[pl.ds(c * RING, RING)].reshape(LINE, 128)
+        state[...] += dot(f_high[c], vc) + dot(f_low[c], vc)
+
+    def on_weights(top, c):
         vc = vbuf[pl.ds(c * RING, RING)].reshape(LINE, 128)
         w = jnp.exp(scores[c] - top)
         total[...] = lanes(jnp.add, total[...], w)
         accum[...] += dot(w.astype(BF16), vc)
-        state[...] += dot(f_high[c], vc) + dot(f_low[c], vc)
+
+    def on_grads(adjoint, a_column, c):
+        kc = kbuf[pl.ds(c * RING, RING)].reshape(LINE, 128)
+        vc = vbuf[pl.ds(c * RING, RING)].reshape(LINE, 128)
+        grad = dot(adjoint[0], vc, NT) + dot(adjoint[1], vc, NT) + a_column
+        f = f_high[c].astype(F32) + f_low[c].astype(F32)
+        back = [features_back(f[i : i + ROWS], grad[i : i + ROWS]) for i in (0, ROWS)]
+        far[...] += dot_left(jnp.concatenate(back, axis=0), kc)
 
     def lines(hop, work):
         @pl.loop(0, 4 if 0 < hop < 4 else 2)
@@ -228,25 +238,15 @@
             def _():
                 work(c)
 
-    lines(0, on_keys)
-    for hop in range(1, 5):
-        pass_on(k_streams, hop)
-        lines(hop, on_keys)
-        if hop < 4:
-            pass_on(v_streams, hop)
-    top = jnp.max(best[...], axis=1, keepdims=True)
-    on_values = functools.partial(on_values, top)
-
     before = jnp.where(y > 0, (RING + y - 1) * RING + z, (2 * RING - 1) * RING + jnp.maximum(z - 1, 0))
     tt, jj = iota((ROWS, 2 * ROWS), 0), iota((ROWS, 2 * ROWS), 1)
     window = (jj > tt) & (jj <= tt + WINDOW) & (bound + jj >= 0)
     tt, jj = iota((ROWS, ROWS), 0), iota((ROWS, ROWS), 1)
     linear_mask = (jj <= tt) & (bound + jj >= 0)
     turned_mask = (tt <= jj) & (bound + tt >= 0)
-    kext = jnp.concatenate([kbuf[before], k_ref[...], k_ref[pl.ds(HALF, HALF)]], axis=0)
-    kf_all = features_of(wk, kext[:ROWS])
-    heads = []
-    for h in range(2):
+
+    def nearby(h):
+        kext = jnp.concatenate([kbuf[before], k_ref[...], k_ref[pl.ds(HALF, HALF)]], axis=0)
         q = queries[h]
         s = dot(q, kext, NT) * scale
         window_best = jnp.max(jnp.where(window, s, LOW), axis=1, keepdims=True)
@@ -254,29 +254,42 @@
         window_total = jnp.sum(weights, axis=1, keepdims=True)
         qft = features_of(three(wq_ref[h]), q)
         qf = qft.T
-        kft = kf_all[h * ROWS : (h + 1) * ROWS]
+        kft = features_of([w[h * HALF : (h + 1) * HALF] for w in wk], kext[:ROWS])
         linear = jnp.where(linear_mask, dot_wide(qf, kft), 0.0)
-        prefix_sum = jnp.sum(state_sum[h * ROWS : (h + 1) * ROWS, :], axis=1, keepdims=True)
-        linear_total = jnp.sum(linear, axis=1, keepdims=True) + dot_wide(
-            qf, jnp.broadcast_to(prefix_sum, (128, 128))
-        )
+        linear_total = jnp.sum(linear, axis=1, keepdims=True)
         lift = jnp.exp(-window_best)
-        inverse = 1.0 / (window_total + lift * linear_total)
-        heads.append((q, weights.astype(BF16), qft, qf, kft, linear, prefix_sum, lift, inverse))
-
+        return q, weights.astype(BF16), window_total, qft, qf, kft, linear, linear_total, lift
+
+    heads = []
+    lines(0, on_keys)
+    lines(0, on_state)
+    for hop in range(1, 5):
+        pass_on(k_streams, hop)
+        lines(hop, on_keys)
+        if hop < 4:
+            pass_on(v_streams, hop)
+            lines(hop, on_state)
+        if 0 < hop < 3:
+            heads.append(nearby(hop - 1))
+    top = jnp.max(best[...], axis=1, keepdims=True)
     for hop in range(4):
-        lines(hop, on_values)
+        lines(hop, functools.partial(on_weights, top))
     pass_on(v_streams, 4)
-    lines(4, on_values)
-
+    lines(4, on_state)
+    lines(4, functools.partial(on_weights, top))
+
+    kext = jnp.concatenate([kbuf[before], k_ref[pl.ds(0, HALF)]], axis=0)
     vext = jnp.concatenate([vbuf[before], v_ref[...], v_ref[pl.ds(HALF, HALF)]], axis=0)
     teacher = accum[...] / jnp.sum(total[...], axis=1, keepdims=True)
     teacher = teacher.astype(BF16).astype(F32)
     loss = jnp.zeros((8, 128), F32)
-    kept = []
+    kept, adjoint, a_column = [], [], []
     for h in range(2):
-        q, weights, qft, qf, kft, linear, prefix_sum, lift, inverse = heads[h]
+        q, weights, window_total, qft, qf, kft, linear, linear_total, lift = heads[h]
         prefix = state[h * ROWS : (h + 1) * ROWS, :]
+        prefix_sum = jnp.sum(state_sum[h * ROWS : (h + 1) * ROWS, :], axis=1, keepdims=True)
+        linear_total = linear_total + dot_wide(qf, jnp.broadcast_to(prefix_sum, (128, 128)))
+        inverse = 1.0 / (window_total + lift * linear_total)
         window_sum = dot(weights, vext)
         linear_sum = dot_left(linear, vext[:ROWS]) + dot_wide(qf, prefix)
         student = (window_sum + lift * linear_sum) * inverse
@@ -288,12 +301,13 @@
         num_grad = lift * grad_out * inverse
         den_grad = -lift * jnp.sum(grad_out * student, axis=1, keepdims=True) * inverse
         dgt = den_grad.T
-        adjoint = dot_wide(qft, num_grad)
-        a_row = dot_wide(jnp.broadcast_to(dgt[:1], (8, ROWS)), qft, NT)
-        for k in range(4):
-            x[4 * h + k, 0:32] = adjoint[32 * k : 32 * (k + 1)]
-            x[4 * h + k, 32:33] = a_row[:1]
-        kept.append((prefix, num_grad, dgt))
+        adjoint.append(dot_wide(qft, num_grad))
+        a_column.append(jnp.sum(qft * dgt[:1], axis=1, keepdims=True))
+        kept.append((prefix, prefix_sum, num_grad, dgt))
+    tile[...] = loss
+    for p in others:
+        remote(tile, tiles.at[xx], send.at[3], recv.at[3, xx], X, p).start()
+    tiles[xx] = loss
 
     def start(k, axis, src, dst):
         for d in FAR_FIRST:
@@ -311,111 +325,75 @@
             out = out + ref[k]
         return out
 
-    start(0, Y, lambda p: x.at[p], b1)
-    b1[y] = x[y]
-    tile[...] = loss
-    for p in others:
-        remote(tile, tiles.at[xx], send.at[1], recv.at[1, xx], X, p).start()
-    tiles[xx] = loss
-
+    near = []
     for h in range(2):
-        q, weights, qft, qf, kft, linear, prefix_sum, lift, inverse = heads[h]
-        prefix, num_grad, dgt = kept[h]
+        q, weights, window_total, qft, qf, kft = heads[h][:6]
+        prefix, prefix_sum, num_grad, dgt = kept[h]
         ngt = num_grad.T
         link = jnp.where(turned_mask, dot_right(vext[:ROWS], ngt) + dgt[:1], 0.0)
         qfg = dot_wide(kft, link) + dot_wide(prefix, ngt) + prefix_sum * dgt[:1]
         kfg = dot_wide(qft, link, NT)
         grad_query = dot_left(features_back(qft, qfg), q)
-        grad_key = dot_left(features_back(kft, kfg), kext[:ROWS])
         for k in range(4):
-            g[4 * h + k, 0:16] = grad_query[16 * k : 16 * (k + 1)]
-            g[4 * h + k, 16:32] = grad_key[16 * k : 16 * (k + 1)]
-    start(2, Z, lambda p: g.at[p], g1)
+            g[4 * h + k] = grad_query[16 * k : 16 * (k + 1)]
+        near.append(dot_left(features_back(kft, kfg), kext))
+    start(0, Z, lambda p: g.at[p], g1)
     g1[z] = g[z]
 
-    own_head, part = jnp.right_shift(y, 2), jnp.bitwise_and(y, 3)
-    sign = jnp.where(part < 2, 1.0, -1.0).astype(F32)
-    within = pl.multiple_of(jnp.bitwise_and(part, 1) * 32, 32)
-    for k in range(RING):
-        if k:
-            at = (RING + k - 1) * RING + z
-        else:
-            at = (2 * RING - 1) * RING + jnp.maximum(z - 1, 0)
-        for row, buf in ((krow, kbuf), (vrow, vbuf)):
-            row[k, 0:HALF] = buf[at]
-            row[k, HALF:ROWS] = buf[z * RING + k]
-    keys_row = krow[...].reshape(RING * ROWS, 128)
-    pieces = three(wk_ref[own_head])
-    act = dot(pieces[0], keys_row, NT) + (dot(pieces[1], keys_row, NT) + dot(pieces[2], keys_row, NT))
-    e = jnp.exp(act * sign)
-    e_row[...] = e * (1.0 / jnp.sum(e, axis=0, keepdims=True))
-
-    finish(0, Y, b1)
-    t1[...] = added(b1)
-    start(3, Z, lambda p: t1, b2)
+    far[...] = jnp.concatenate(near, axis=0)
+    work = functools.partial(
+        on_grads, two(jnp.concatenate(adjoint, axis=0)), jnp.concatenate(a_column, axis=0)
+    )
+    for hop in range(5):
+        lines(hop, work)
+    for h in range(2):
+        for k in range(RING):
+            gk[h, k] = far[h * HALF + 8 * k : h * HALF + 8 * (k + 1)]
+
+    ways = ((Y, Z, y, z), (Z, Y, z, y))
+    for h, (one, other, mine, across) in enumerate(ways):
+        start(6 + h, one, lambda p, h=h: gk.at[h, p], k1.at[h])
+        k1[h, mine] = gk[h, mine]
     for p in others:
-        remote(tile, tiles.at[p], send.at[1], recv.at[1, p], X, p).wait_recv()
+        remote(tile, tiles.at[p], send.at[3], recv.at[3, p], X, p).wait_recv()
     tile_x[...] = added(tiles, 0, 4)
     start(4, Z, lambda p: tile_x, l1)
     l1[z] = tile_x[...]
-    finish(2, Z, g1)
+    finish(0, Z, g1)
     g1s[...] = added(g1)
-    start(5, Y, lambda p: g1s, g2)
+    start(1, Y, lambda p: g1s, g2)
     g2[y] = g1s[...]
-    b2[z] = t1[...]
-    finish(3, Z, b2)
-
-    base = jnp.zeros((33, 128), F32)
-    for k in range(1, RING):
-        base = base + jnp.where(k > z, b2[k], 0.0)
-    for k in reversed(range(RING)):
-        suffix[k] = base
-        arows[k : k + 1, :] = base[32:33]
-        base = base + b1[k]
-    acol[...] = arows[...].T
-    columns = acol[pl.ds(pl.multiple_of(part * 32, 32), 32), :]
-    grads = []
-    for k in range(RING):
-        grads.append(dot_left(suffix[k, 0:32], vrow[k], NT) + columns[:, k : k + 1])
-    weighted = jnp.concatenate(grads, axis=1) * e_row[pl.ds(within, 32), :]
-    kag[...] = -e_row[...] * jnp.sum(weighted, axis=0, keepdims=True)
-    kag[pl.ds(within, 32), :] += weighted
-    real = (iota((1, RING * ROWS), 1) >= HALF) | (z > 0)
-    far = dot_left(jnp.where(real, kag[...] * sign, 0.0), keys_row)
-    for k in range(RING):
-        gp[k] = far[8 * k : 8 * (k + 1)]
-    start(6, Z, lambda p: gp.at[p], ba)
-    ba[z] = gp[z]
-
-    finish(5, Y, g2)
-    g2s[...] = added(g2)
-    start(7, Z, lambda p: g2s, out_g)
-    out_g[z] = g2s[...]
+    for h, (one, other, mine, across) in enumerate(ways):
+        finish(6 + h, one, k1.at[h])
+        k1s[h] = added(k1[h])
+        start(8 + h, other, lambda p, h=h: k1s.at[h], k2.at[h])
+        k2[h, across] = k1s[h]
     finish(4, Z, l1)
     l1s[...] = added(l1)
-    start(8, Y, lambda p: l1s, l2)
+    start(5, Y, lambda p: l1s, l2)
     l2[y] = l1s[...]
-
-    finish(6, Z, ba)
-    bas[...] = added(ba)
-    start(9, Y, lambda p: bas, bb)
-    bb[y] = bas[...]
-    finish(9, Y, bb)
-    bbs[0:8] = added(bb, 0, 4)
-    bbs[8:16] = added(bb, 4, 8)
-    start(10, Z, lambda p: bbs, out_k)
-    out_k[z] = bbs[...]
-    finish(8, Y, l2)
+    finish(1, Y, g2)
+    g2s[...] = added(g2)
+    start(2, Z, lambda p: g2s, out_g)
+    out_g[z] = g2s[...]
+    for h, (one, other, mine, across) in enumerate(ways):
+        finish(8 + h, other, k2.at[h])
+        k2s[h] = added(k2[h])
+        start(10 + h, one, lambda p, h=h: k2s.at[h], out_k.at[h])
+        out_k[h, mine] = k2s[h]
+    finish(5, Y, l2)
     out_loss[...] = added(l2)
-    finish(7, Z, out_g)
-    finish(10, Z, out_k)
+    finish(2, Z, out_g)
+    for h, (one, other, mine, across) in enumerate(ways):
+        finish(10 + h, one, out_k.at[h])
 
     for stream in k_streams + v_streams:
         sent = stream[0].at[pl.ds(0, RING * RING - 1)]
         remote(sent, sent, stream[1], stream[2].at[0], Z, z).wait_send()
     for k, ref, count in (
-        (0, b1, 7), (1, tiles, 3), (2, g1, 7), (3, b2, 7), (4, l1, 7), (5, g2, 7),
-        (6, ba, 7), (7, out_g, 7), (8, l2, 7), (9, bb, 7), (10, out_k, 7),
+        (0, g1, 7), (1, g2, 7), (2, out_g, 7), (3, tiles, 3), (4, l1, 7), (5, l2, 7),
+        (6, k1.at[0], 7), (7, k1.at[1], 7), (8, k2.at[0], 7), (9, k2.at[1], 7),
+        (10, out_k.at[0], 7), (11, out_k.at[1], 7),
     ):
         sent = ref.at[pl.ds(0, count)]
         remote(sent, sent, send.at[k], recv.at[k, 0], Z, z).wait_send()
@@ -438,16 +416,14 @@
     scratch = [
         blocks, blocks, f32(16, 256, LINE), bf16(16, 256, LINE), bf16(16, 256, LINE),
         f32(256, 128), f32(256, 128), f32(256, 128), f32(256, 128), f32(256, 128),
-        bf16(8, 128, 128), bf16(8, 128, 128), f32(64, 1024), f32(64, 1024), f32(8, 128), f32(128, 8),
-        f32(8, 33, 128), f32(8, 33, 128), f32(33, 128), f32(8, 33, 128), f32(8, 33, 128),
-        f32(8, 32, 128), f32(8, 32, 128), f32(32, 128), f32(8, 32, 128), f32(32, 128),
+        f32(128, 128), f32(8, 16, 128), f32(8, 16, 128), f32(16, 128), f32(8, 16, 128), f32(16, 128),
         f32(8, 128), f32(4, 8, 128), f32(8, 128), f32(8, 8, 128), f32(8, 128), f32(8, 8, 128),
-        f32(8, 8, 128), f32(8, 8, 128), f32(8, 128), f32(8, 8, 128), f32(16, 128),
-        dma((4,)), dma((128,)), dma((128,)), dma((11,)), dma((11, RING)),
+        f32(2, 8, 8, 128), f32(2, 8, 8, 128), f32(2, 8, 128), f32(2, 8, 8, 128), f32(2, 8, 128),
+        dma((4,)), dma((128,)), dma((128,)), dma((12,)), dma((12, RING)),
     ]
     return pl.pallas_call(
         layer_kernel,
-        out_shape=(shape((8, 32, 128), F32), shape((8, 16, 128), F32), shape((8, 128), F32)),
+        out_shape=(shape((8, 16, 128), F32), shape((2, 8, 8, 128), F32), shape((8, 128), F32)),
         in_specs=[VMEM] * 5,
         out_specs=(VMEM,) * 3,
         scratch_shapes=scratch,
@@ -460,10 +436,8 @@
 
 def finish_kernel(g_ref, k_ref, loss_ref, loss, grad_query, grad_key):
     loss[0] = jnp.sum(loss_ref[...]) * (1.0 / TOKENS)
-    grad_query[...] = g_ref[:, 0:16].reshape(2, HALF, 128)
-    near = g_ref[:, 16:32].reshape(2, HALF, 128)
-    for h in range(2):
-        grad_key[h] = near[h] + k_ref[:, 8 * h : 8 * (h + 1)].reshape(HALF, 128)
+    grad_query[...] = g_ref[...].reshape(2, HALF, 128)
+    grad_key[...] = k_ref[...].reshape(2, HALF, 128)
 
 
 def local(queries, keys, values, query_weight, key_weight):

time: 80.5 us -> 75.7 us (0.940)
  Pallas kernels: 79.6 us -> 74.9 us
    pallas_call x1, Pallas kernels: 77.9 us -> 73.3 us  [layer(): pl.pallas_call(layer_kernel, out_shape=(shape((8, 16, 128), F32), shape((...]
where the time goes in v4:
time: 75.7 us; the launch traced here: 75.5 us
  Pallas kernels  74.9 us (99%)
    pallas_call x1, Pallas kernels, layer(): pl.pallas_call(layer_kernel, out_shape=(shape((8, 16, 128), F32), shape((...  73.3 us
    pallas_call x1, Pallas kernels, local(): pl.pallas_call(finish_kernel, out_shape=(shape((1,), F32), shape(query_we...  1.54 us

profile of v4, /device:TPU:6, one launch (start us, length us, event | category | flops | bytes accessed | tf_op | source)
XLA Modules:
  0.0 75.5 jit_solution(4762419017322642340)
XLA Ops:
  0.6 73.3 %layer.1 = (f32[8,16,128]{2,1,0:T(8,128)}, f32[2,8,8,128]{3,2,1,0:T(8,128)}, f32[8,128]{1,0:T(8,128)}) custom-call(bf16[128,2,128]{2,1,0:T(2,128)(2,1)} %q_ref.1, bf16[128,128]{1,0:T(8,128)(2,1)} %k_ref.1, bf16[128,128]{1,0:T(8,128)(2,1)} %v_ref.1, f32[2,64,128]{2,1,0:T(8,128)} %wq_ref.1, f32[2,64,128]{2,1,0:T(8,128)} %wk_ref.1), custom_call_target="tpu_custom_call" | custom-call | tf_op jit(solution)/shard_map/layer/pallas_call | solution.py:424
  74.0 1.5 %finish.1 = (f32[1]{0:T(128)}, f32[2,64,128]{2,1,0:T(8,128)}, f32[2,64,128]{2,1,0:T(8,128)}) custom-call(f32[8,16,128]{2,1,0:T(8,128)} %get-tuple-element.6.g_ref, f32[2,8,8,128]{3,2,1,0:T(8,128)} %get-tuple-element.7.k_ref, f32[8,128]{1,0:T(8,128)} %get-tuple-element.8.loss_ref), custom_call_target="tpu_custom_call" | custom-call | tf_op jit(solution)/shard_map/finish/pallas_call | solution.py:445

commit v5 on v4

--- a/solution.py
+++ b/solution.py
@@ -195,48 +195,54 @@
             start = fold(start, value[:, k * 128 : (k + 1) * 128])
         return start
 
-    def on_keys(c):
-        line = jnp.bitwise_and(c, RING - 1)
-        second = c >= RING
-        at = jnp.where(second, line * ROWS + HALF, line * (ROWS * RING))
-        at = at + lane_block * jnp.where(second, ROWS * RING, ROWS) + lane_row
-        kc = kbuf[pl.ds(c * RING, RING)].reshape(LINE, 128)
-        s = dot(q_all, kc, NT) * scale
-        s = jnp.where(at <= query_place, s, LOW)
-        scores[c] = s
-        best[...] = lanes(jnp.maximum, best[...], s)
-        f = jnp.where(at < bound, features_of(wk, kc), 0.0)
-        state_sum[...] = lanes(jnp.add, state_sum[...], f)
-        f_high[c], f_low[c] = two(f)
-
-    def on_state(c):
-        vc = vbuf[pl.ds(c * RING, RING)].reshape(LINE, 128)
-        state[...] += dot(f_high[c], vc) + dot(f_low[c], vc)
-
-    def on_weights(top, c):
-        vc = vbuf[pl.ds(c * RING, RING)].reshape(LINE, 128)
-        w = jnp.exp(scores[c] - top)
-        total[...] = lanes(jnp.add, total[...], w)
-        accum[...] += dot(w.astype(BF16), vc)
-
-    def on_grads(adjoint, a_column, c):
-        kc = kbuf[pl.ds(c * RING, RING)].reshape(LINE, 128)
-        vc = vbuf[pl.ds(c * RING, RING)].reshape(LINE, 128)
-        grad = dot(adjoint[0], vc, NT) + dot(adjoint[1], vc, NT) + a_column
-        f = f_high[c].astype(F32) + f_low[c].astype(F32)
-        back = [features_back(f[i : i + ROWS], grad[i : i + ROWS]) for i in (0, ROWS)]
-        far[...] += dot_left(jnp.concatenate(back, axis=0), kc)
+    def chunk(buf, c):
+        return buf[pl.ds(c * RING, RING)].reshape(LINE, 128)
+
+    def on_keys(cs):
+        top, sums = best[...], state_sum[...]
+        for c in cs:
+            line = jnp.bitwise_and(c, RING - 1)
+            second = c >= RING
+            at = jnp.where(second, line * ROWS + HALF, line * (ROWS * RING))
+            at = at + lane_block * jnp.where(second, ROWS * RING, ROWS) + lane_row
+            kc = chunk(kbuf, c)
+            s = dot(q_all, kc, NT) * scale
+            s = jnp.where(at <= query_place, s, LOW)
+            scores[c] = s
+            top = lanes(jnp.maximum, top, s)
+            f = jnp.where(at < bound, features_of(wk, kc), 0.0)
+            sums = lanes(jnp.add, sums, f)
+            f_high[c], f_low[c] = two(f)
+        best[...], state_sum[...] = top, sums
+
+    def on_state(cs):
+        add = state[...]
+        for c in cs:
+            vc = chunk(vbuf, c)
+            add = add + (dot(f_high[c], vc) + dot(f_low[c], vc))
+        state[...] = add
+
+    def on_weights(top, cs):
+        sums, add = total[...], accum[...]
+        for c in cs:
+            w = jnp.exp(scores[c] - top)
+            sums = lanes(jnp.add, sums, w)
+            add = add + dot(w.astype(BF16), chunk(vbuf, c))
+        total[...], accum[...] = sums, add
+
+    def on_grads(adjoint, a_column, cs):
+        add = far[...]
+        for c in cs:
+            vc = chunk(vbuf, c)
+            grad = dot(adjoint[0], vc, NT) + dot(adjoint[1], vc, NT) + a_column
+            f = f_high[c].astype(F32) + f_low[c].astype(F32)
+            back = [features_back(f[i : i + ROWS], grad[i : i + ROWS]) for i in (0, ROWS)]
+            add = add + dot_left(jnp.concatenate(back, axis=0), chunk(kbuf, c))
+        far[...] = add
 
     def lines(hop, work):
-        @pl.loop(0, 4 if 0 < hop < 4 else 2)
-        def _(i):
-            second = jnp.bitwise_and(i, 1)
-            steps = jnp.where(i < 2, RING - hop, RING + hop)
-            c = second * RING + lax.rem(jnp.where(second == 1, y, z) + steps, RING)
-
-            @pl.when(jnp.logical_or(second == 1, c <= z))
-            def _():
-                work(c)
+        ways = (hop,) if hop in (0, 4) else (-hop, hop)
+        work([c for way in ways for c in (around(z, way), RING + around(y, way))])
 
     before = jnp.where(y > 0, (RING + y - 1) * RING + z, (2 * RING - 1) * RING + jnp.maximum(z - 1, 0))
     tt, jj = iota((ROWS, 2 * ROWS), 0), iota((ROWS, 2 * ROWS), 1)

time: 75.7 us -> 71.8 us (0.948)
  Pallas kernels: 74.9 us -> 70.7 us
    pallas_call x1, Pallas kernels: 73.3 us -> 69.2 us  [layer(): pl.pallas_call(layer_kernel, out_shape=(shape((8, 16, 128), F32), shape((...]
where the time goes in v5:
time: 71.8 us; the launch traced here: 71.5 us
  Pallas kernels  70.7 us (98%)
  between operations  0.8 us (1%)
    pallas_call x1, Pallas kernels, layer(): pl.pallas_call(layer_kernel, out_shape=(shape((8, 16, 128), F32), shape((...  69.2 us
    pallas_call x1, Pallas kernels, local(): pl.pallas_call(finish_kernel, out_shape=(shape((1,), F32), shape(query_we...  1.54 us

profile of v5, /device:TPU:6, one launch (start us, length us, event | category | flops | bytes accessed | tf_op | source)
XLA Modules:
  0.0 71.5 jit_solution(10507902279292652596)
XLA Ops:
  0.6 69.2 %layer.1 = (f32[8,16,128]{2,1,0:T(8,128)}, f32[2,8,8,128]{3,2,1,0:T(8,128)}, f32[8,128]{1,0:T(8,128)}) custom-call(bf16[128,2,128]{2,1,0:T(2,128)(2,1)} %q_ref.1, bf16[128,128]{1,0:T(8,128)(2,1)} %k_ref.1, bf16[128,128]{1,0:T(8,128)(2,1)} %v_ref.1, f32[2,64,128]{2,1,0:T(8,128)} %wq_ref.1, f32[2,64,128]{2,1,0:T(8,128)} %wk_ref.1), custom_call_target="tpu_custom_call" | custom-call | tf_op jit(solution)/shard_map/layer/pallas_call | solution.py:430
  69.8 1.5 %finish.1 = (f32[1]{0:T(128)}, f32[2,64,128]{2,1,0:T(8,128)}, f32[2,64,128]{2,1,0:T(8,128)}) custom-call(f32[8,16,128]{2,1,0:T(8,128)} %get-tuple-element.6.g_ref, f32[2,8,8,128]{3,2,1,0:T(8,128)} %get-tuple-element.7.k_ref, f32[8,128]{1,0:T(8,128)} %get-tuple-element.8.loss_ref), custom_call_target="tpu_custom_call" | custom-call | tf_op jit(solution)/shard_map/finish/pallas_call | solution.py:451

commit v6 on v5

--- a/solution.py
+++ b/solution.py
@@ -78,7 +78,7 @@
 
 
 def features_of(pieces, tokens):
-    act = dot(pieces[0], tokens, NT) + (dot(pieces[1], tokens, NT) + dot(pieces[2], tokens, NT))
+    act = sum(dot(piece, tokens, NT) for piece in pieces[1:]) + dot(pieces[0], tokens, NT)
     half = 64
     parts = []
     for h in range(act.shape[0] // half):
@@ -119,7 +119,8 @@
     me = z * RING + y
     place = {Z: z, Y: y}
     others = [lax.rem(xx + d, 4) for d in (2, 1, 3)]
-    greet([(axis, around(place[axis], d)) for d in FAR_FIRST for axis in (Z, Y)] + [(X, p) for p in others])
+    close = [(axis, around(place[axis], d)) for d in (2, -2, 1, -1) for axis in (Z, Y)]
+    greet(close + [(X, p) for p in others])
 
     k_streams = ((kbuf, kv_send.at[0], k_recv, 0, Y, Z), (kbuf, kv_send.at[1], k_recv, 1, Z, Y))
     v_streams = ((vbuf, kv_send.at[2], v_recv, 0, Y, Z), (vbuf, kv_send.at[3], v_recv, 1, Z, Y))
@@ -145,7 +146,7 @@
         for way in (1, -1):
             push(stream, src, at, stream[5], way)
     for ref, streams in ((k_ref, k_streams), (v_ref, v_streams)):
-        for step in (1, 7, 4, 3, 5, 2, 6):
+        for step in (1, -1, 2, -2):
             for stream in streams:
                 push(stream, ref.at[halves[stream[3]]], piece(stream, 0, 0), stream[4], step)
     for stream in v_streams:
@@ -163,13 +164,27 @@
     q_all = jnp.concatenate(queries, axis=0)
     wk = three(wk_ref[...].reshape(2 * HALF, 128))
 
-    for streams in (k_streams, v_streams):
-        for along in NEAR_FIRST:
-            for stream in streams:
-                at = piece(stream, along, 0)
-                arrived(stream, at)
-                forward(stream, at, stream[5], 1)
-                forward(stream, at, stream[5], -1)
+    query_features = []
+    for h in range(2):
+        qft = features_of(three(wq_ref[h]), queries[h])
+        query_features.append((qft, qft.T))
+
+    for offsets in ((-1, 1, -2, 2), (-3, 3, 4)):
+        for streams in (k_streams, v_streams):
+            for along in offsets:
+                for stream in streams:
+                    at = piece(stream, along, 0)
+                    arrived(stream, at)
+                    if along == -2:
+                        forward(stream, at, stream[4], 1)
+                        if streams is k_streams:
+                            forward(stream, at, stream[4], 2)
+                    if along == 2:
+                        forward(stream, at, stream[4], -1)
+                        if streams is v_streams:
+                            forward(stream, at, stream[4], -2)
+                    forward(stream, at, stream[5], 1)
+                    forward(stream, at, stream[5], -1)
 
     def pass_on(streams, hop):
         for along in (0, -1, 1, -2, 2, -3, 3, 4):
@@ -210,7 +225,7 @@
             s = jnp.where(at <= query_place, s, LOW)
             scores[c] = s
             top = lanes(jnp.maximum, top, s)
-            f = jnp.where(at < bound, features_of(wk, kc), 0.0)
+            f = jnp.where(at < bound, features_of(wk[:2], kc), 0.0)
             sums = lanes(jnp.add, sums, f)
             f_high[c], f_low[c] = two(f)
         best[...], state_sum[...] = top, sums
@@ -258,46 +273,52 @@
         window_best = jnp.max(jnp.where(window, s, LOW), axis=1, keepdims=True)
         weights = jnp.where(window, jnp.exp(s - window_best), 0.0)
         window_total = jnp.sum(weights, axis=1, keepdims=True)
-        qft = features_of(three(wq_ref[h]), q)
-        qf = qft.T
+        qft, qf = query_features[h]
         kft = features_of([w[h * HALF : (h + 1) * HALF] for w in wk], kext[:ROWS])
         linear = jnp.where(linear_mask, dot_wide(qf, kft), 0.0)
         linear_total = jnp.sum(linear, axis=1, keepdims=True)
         lift = jnp.exp(-window_best)
         return q, weights.astype(BF16), window_total, qft, qf, kft, linear, linear_total, lift
 
+    def ready(h, head):
+        q, weights, window_total, qft, qf, kft, linear, linear_total, lift = head
+        vext = jnp.concatenate([vbuf[before], v_ref[...], v_ref[pl.ds(HALF, HALF)]], axis=0)
+        prefix_sum = jnp.sum(state_sum[h * ROWS : (h + 1) * ROWS, :], axis=1, keepdims=True)
+        linear_total = linear_total + dot_wide(qf, jnp.broadcast_to(prefix_sum, (128, 128)))
+        inverse = 1.0 / (window_total + lift * linear_total)
+        return q, qft, qf, kft, prefix_sum, lift, inverse, dot(weights, vext), dot_left(linear, vext[:ROWS])
+
     heads = []
     lines(0, on_keys)
     lines(0, on_state)
-    for hop in range(1, 5):
+    for hop in (1, 2, 3):
         pass_on(k_streams, hop)
         lines(hop, on_keys)
-        if hop < 4:
-            pass_on(v_streams, hop)
-            lines(hop, on_state)
-        if 0 < hop < 3:
+        pass_on(v_streams, hop)
+        lines(hop, on_state)
+        if hop < 3:
             heads.append(nearby(hop - 1))
+    pass_on(k_streams, 4)
+    lines(4, on_keys)
     top = jnp.max(best[...], axis=1, keepdims=True)
+    on_weights = functools.partial(on_weights, top)
     for hop in range(4):
-        lines(hop, functools.partial(on_weights, top))
+        lines(hop, on_weights)
+    heads = [ready(h, heads[h]) for h in range(2)]
     pass_on(v_streams, 4)
     lines(4, on_state)
-    lines(4, functools.partial(on_weights, top))
+    lines(4, on_weights)
 
     kext = jnp.concatenate([kbuf[before], k_ref[pl.ds(0, HALF)]], axis=0)
-    vext = jnp.concatenate([vbuf[before], v_ref[...], v_ref[pl.ds(HALF, HALF)]], axis=0)
+    vext = jnp.concatenate([vbuf[before], v_ref[pl.ds(0, HALF)]], axis=0)
     teacher = accum[...] / jnp.sum(total[...], axis=1, keepdims=True)
     teacher = teacher.astype(BF16).astype(F32)
     loss = jnp.zeros((8, 128), F32)
     kept, adjoint, a_column = [], [], []
     for h in range(2):
-        q, weights, window_total, qft, qf, kft, linear, linear_total, lift = heads[h]
+        q, qft, qf, kft, prefix_sum, lift, inverse, window_sum, linear_sum = heads[h]
         prefix = state[h * ROWS : (h + 1) * ROWS, :]
-        prefix_sum = jnp.sum(state_sum[h * ROWS : (h + 1) * ROWS, :], axis=1, keepdims=True)
-        linear_total = linear_total + dot_wide(qf, jnp.broadcast_to(prefix_sum, (128, 128)))
-        inverse = 1.0 / (window_total + lift * linear_total)
-        window_sum = dot(weights, vext)
-        linear_sum = dot_left(linear, vext[:ROWS]) + dot_wide(qf, prefix)
+        linear_sum = linear_sum + dot_wide(qf, prefix)
         student = (window_sum + lift * linear_sum) * inverse
         difference = student - teacher[h * ROWS : (h + 1) * ROWS]
         square = difference * difference
@@ -309,7 +330,7 @@
         dgt = den_grad.T
         adjoint.append(dot_wide(qft, num_grad))
         a_column.append(jnp.sum(qft * dgt[:1], axis=1, keepdims=True))
-        kept.append((prefix, prefix_sum, num_grad, dgt))
+        kept.append((prefix, num_grad, dgt))
     tile[...] = loss
     for p in others:
         remote(tile, tiles.at[xx], send.at[3], recv.at[3, xx], X, p).start()
@@ -333,25 +354,29 @@
 
     near = []
     for h in range(2):
-        q, weights, window_total, qft, qf, kft = heads[h][:6]
-        prefix, prefix_sum, num_grad, dgt = kept[h]
+        q, qft, qf, kft, prefix_sum = heads[h][:5]
+        prefix, num_grad, dgt = kept[h]
         ngt = num_grad.T
-        link = jnp.where(turned_mask, dot_right(vext[:ROWS], ngt) + dgt[:1], 0.0)
+        link = jnp.where(turned_mask, dot_right(vext, ngt) + dgt[:1], 0.0)
         qfg = dot_wide(kft, link) + dot_wide(prefix, ngt) + prefix_sum * dgt[:1]
         kfg = dot_wide(qft, link, NT)
         grad_query = dot_left(features_back(qft, qfg), q)
-        for k in range(4):
-            g[4 * h + k] = grad_query[16 * k : 16 * (k + 1)]
+        queries[h] = grad_query
         near.append(dot_left(features_back(kft, kfg), kext))
-    start(0, Z, lambda p: g.at[p], g1)
-    g1[z] = g[z]
-
-    far[...] = jnp.concatenate(near, axis=0)
+    far[...] = jnp.zeros_like(far)
     work = functools.partial(
         on_grads, two(jnp.concatenate(adjoint, axis=0)), jnp.concatenate(a_column, axis=0)
     )
-    for hop in range(5):
+    lines(0, work)
+    lines(1, work)
+    for h in range(2):
+        for k in range(4):
+            g[4 * h + k] = queries[h][16 * k : 16 * (k + 1)]
+    start(0, Z, lambda p: g.at[p], g1)
+    g1[z] = g[z]
+    for hop in range(2, 5):
         lines(hop, work)
+    far[...] += jnp.concatenate(near, axis=0)
     for h in range(2):
         for k in range(RING):
             gk[h, k] = far[h * HALF + 8 * k : h * HALF + 8 * (k + 1)]

time: 71.8 us -> 71.2 us (level)
  Pallas kernels: 70.7 us -> 69.9 us
    pallas_call x1, Pallas kernels: 69.2 us -> 68.4 us  [layer(): pl.pallas_call(layer_kernel, out_shape=(shape((8, 16, 128), F32), shape((...]
where the time goes in v6:
time: 71.2 us; the launch traced here: 70.7 us
  Pallas kernels  69.9 us (98%)
  between operations  0.8 us (1%)
    pallas_call x1, Pallas kernels, layer(): pl.pallas_call(layer_kernel, out_shape=(shape((8, 16, 128), F32), shape((...  68.4 us
    pallas_call x1, Pallas kernels, local(): pl.pallas_call(finish_kernel, out_shape=(shape((1,), F32), shape(query_we...  1.54 us

profile of v6, /device:TPU:6, one launch (start us, length us, event | category | flops | bytes accessed | tf_op | source)
XLA Modules:
  0.0 70.7 jit_solution(10617569344343209233)
XLA Ops:
  0.6 68.4 %layer.1 = (f32[8,16,128]{2,1,0:T(8,128)}, f32[2,8,8,128]{3,2,1,0:T(8,128)}, f32[8,128]{1,0:T(8,128)}) custom-call(bf16[128,2,128]{2,1,0:T(2,128)(2,1)} %q_ref.1, bf16[128,128]{1,0:T(8,128)(2,1)} %k_ref.1, bf16[128,128]{1,0:T(8,128)(2,1)} %v_ref.1, f32[2,64,128]{2,1,0:T(8,128)} %wq_ref.1, f32[2,64,128]{2,1,0:T(8,128)} %wk_ref.1), custom_call_target="tpu_custom_call" | custom-call | tf_op jit(solution)/shard_map/layer/pallas_call | solution.py:455
  69.0 1.5 %finish.1 = (f32[1]{0:T(128)}, f32[2,64,128]{2,1,0:T(8,128)}, f32[2,64,128]{2,1,0:T(8,128)}) custom-call(f32[8,16,128]{2,1,0:T(8,128)} %get-tuple-element.6.g_ref, f32[2,8,8,128]{3,2,1,0:T(8,128)} %get-tuple-element.7.k_ref, f32[8,128]{1,0:T(8,128)} %get-tuple-element.8.loss_ref), custom_call_target="tpu_custom_call" | custom-call | tf_op jit(solution)/shard_map/finish/pallas_call | solution.py:476

commit v7 on v6

--- a/solution.py
+++ b/solution.py
@@ -293,8 +293,8 @@
     lines(0, on_state)
     for hop in (1, 2, 3):
         pass_on(k_streams, hop)
+        pass_on(v_streams, hop)
         lines(hop, on_keys)
-        pass_on(v_streams, hop)
         lines(hop, on_state)
         if hop < 3:
             heads.append(nearby(hop - 1))

time: 71.2 us -> 72.2 us (1.014)
  no operation moved by 1% of the time
where the time goes in v7:
time: 72.2 us; the launch traced here: 71.4 us
  Pallas kernels  70.6 us (98%)
  between operations  0.8 us (1%)
    pallas_call x1, Pallas kernels, layer(): pl.pallas_call(layer_kernel, out_shape=(shape((8, 16, 128), F32), shape((...  69.1 us
    pallas_call x1, Pallas kernels, local(): pl.pallas_call(finish_kernel, out_shape=(shape((1,), F32), shape(query_we...  1.54 us

profile of v7, /device:TPU:6, one launch (start us, length us, event | category | flops | bytes accessed | tf_op | source)
XLA Modules:
  0.0 71.4 jit_solution(7256177837085590898)
XLA Ops:
  0.6 69.1 %layer.1 = (f32[8,16,128]{2,1,0:T(8,128)}, f32[2,8,8,128]{3,2,1,0:T(8,128)}, f32[8,128]{1,0:T(8,128)}) custom-call(bf16[128,2,128]{2,1,0:T(2,128)(2,1)} %q_ref.1, bf16[128,128]{1,0:T(8,128)(2,1)} %k_ref.1, bf16[128,128]{1,0:T(8,128)(2,1)} %v_ref.1, f32[2,64,128]{2,1,0:T(8,128)} %wq_ref.1, f32[2,64,128]{2,1,0:T(8,128)} %wk_ref.1), custom_call_target="tpu_custom_call" | custom-call | tf_op jit(solution)/shard_map/layer/pallas_call | solution.py:455
  69.7 1.5 %finish.1 = (f32[1]{0:T(128)}, f32[2,64,128]{2,1,0:T(8,128)}, f32[2,64,128]{2,1,0:T(8,128)}) custom-call(f32[8,16,128]{2,1,0:T(8,128)} %get-tuple-element.6.g_ref, f32[2,8,8,128]{3,2,1,0:T(8,128)} %get-tuple-element.7.k_ref, f32[8,128]{1,0:T(8,128)} %get-tuple-element.8.loss_ref), custom_call_target="tpu_custom_call" | custom-call | tf_op jit(solution)/shard_map/finish/pallas_call | solution.py:476
